TPU v7x, 16 devices: a whole 2x2x2 slice. The times are simulated.
16 devices in a mesh: col: 4 (over z, y), row: 4 (over x, core).
Axes of the slice: x: 2, y: 2, z: 2, core: 2. Of those that a mesh axis runs over, the one named last changes fastest.
Arguments:
- hyper_params: float32 [3], replicated
- w_in: float32 [2, 2560, 6720], P(None, 'row', 'col')
- x_in: bfloat16 [2, 2048, 2560], P(None, None, 'row')
- dy_in: bfloat16 [2, 2048, 6720], P(None, None, 'col')
- row_in: float32 [2, 2560], P(None, 'row')
- col_in: float32 [2, 6720], P(None, 'col')
- w_out: float32 [2, 6720, 2560], P(None, 'col', 'row')
- x_out: bfloat16 [2, 2048, 6720], P(None, None, 'col')
- dy_out: bfloat16 [2, 2048, 2560], P(None, None, 'row')
- row_out: float32 [2, 6720], P(None, 'col')
- col_out: float32 [2, 2560], P(None, 'row')
Outputs:
- output 1: float32 [2, 2560, 6720], P(None, 'row', 'col')
- output 2: float32 [2, 2560], P(None, 'row')
- output 3: float32 [2, 6720], P(None, 'col')
- output 4: float32 [2, 6720, 2560], P(None, 'col', 'row')
- output 5: float32 [2, 6720], P(None, 'col')
- output 6: float32 [2, 2560], P(None, 'row')
All inputs are finite; a program needn't handle non-finite values.
Results may differ from a plain program's by a relative error of at most 0.001.
Values are sent between devices in bfloat16 or wider.
A program may use at most 1 GiB of HBM per device.

v0:
```python
import functools

import jax
import jax.numpy as jnp
from jax import lax
from jax.experimental import pallas as pl
from jax.experimental.pallas import tpu as pltpu
from jax.sharding import PartitionSpec as P

EPS_ONE = 1e-30
EPS_TWO = 1e-3
MESH = pl.DeviceIdType.MESH
F32 = jnp.float32
LANES = 128


def col_tiles(width):
    return [(start, min(LANES, width - start)) for start in range(0, width, LANES)]


def stats_kernel(n_col, n_row, chunk, hyper, w_in, x_in, dy_in, row_in, col_in, w_out, x_out, dy_out, row_out, col_out,
                 wv_in, row_in_new, col_in_new, wv_out, row_out_new, col_out_new,
                 upd, a_buf, b_buf, row_acc, col_acc, w_col, rx_n, rx_w, rx_s, old_n, old_w, new_narrow, new_wide,
                 a_sem, b_sem, w_sem, send_n, recv_n, send_w, recv_w, send_s, recv_s):
    n_mat, wide, narrow = upd.shape
    layers = n_mat // 2
    full_narrow, full_wide = narrow * n_row, wide * n_col
    n_total = float(full_narrow * full_wide)
    my_c, my_r = lax.axis_index("col"), lax.axis_index("row")
    n_dev = n_col * n_row
    me = my_c * n_row + my_r
    tiles = col_tiles(wide)
    nt = col_tiles(narrow)

    def loads(m, slot):
        layer = lax.rem(m, layers)

        def pair(a_src, b_src):
            return (pltpu.make_async_copy(a_src.at[layer], a_buf.at[slot], a_sem.at[slot]),
                    pltpu.make_async_copy(b_src.at[layer], b_buf.at[slot], b_sem.at[slot]))
        return pair(x_in, dy_in), pair(dy_out, x_out)

    def start_loads(m, slot):
        first, second = loads(m, slot)

        @pl.when(m < layers)
        def _():
            for copy in first:
                copy.start()

        @pl.when(m >= layers)
        def _():
            for copy in second:
                copy.start()

    start_loads(jnp.int32(0), 0)
    barrier = pltpu.get_barrier_semaphore()
    for d in range(1, n_dev):
        peer = lax.rem(me + d, n_dev)
        pl.semaphore_signal(barrier, inc=1, device_id=(peer // n_row, lax.rem(peer, n_row)), device_id_type=MESH)

    old_n[...] = jnp.zeros_like(old_n)
    old_w[...] = jnp.zeros_like(old_w)
    for m in range(n_mat):
        rx_n[m, my_c] = jnp.zeros(rx_n.shape[2:], F32)
        rx_w[m, my_r] = jnp.zeros(rx_w.shape[2:], F32)
    for layer in range(layers):
        for m, src_n, src_w in ((layer, row_in, col_in), (layers + layer, col_out, row_out)):
            for j, (s, w) in enumerate(nt):
                old_n[m, j:j + 1, :w] = src_n[layer:layer + 1, s:s + w]
            for j, (s, w) in enumerate(tiles):
                old_w[m, j:j + 1, :w] = src_w[layer:layer + 1, s:s + w]
    pl.semaphore_wait(barrier, n_dev - 1)

    w_copies = ([pltpu.make_async_copy(w_in.at[i], wv_in.at[i], w_sem.at[i]) for i in range(layers)]
                + [pltpu.make_async_copy(w_out.at[i], wv_out.at[i], w_sem.at[layers + i]) for i in range(layers)])

    def on_weights(m, fn):
        @pl.when(m < layers)
        def _():
            fn(wv_in)

        @pl.when(m >= layers)
        def _():
            fn(wv_out)

    def narrow_copy(m, d):
        peer = lax.rem(my_c + d, n_col)
        return pltpu.make_async_remote_copy(
            src_ref=rx_n.at[m, my_c], dst_ref=rx_n.at[m, my_c], send_sem=send_n.at[m, d], recv_sem=recv_n.at[m, my_c],
            device_id=(peer, my_r), device_id_type=MESH)

    def narrow_arrival(m, d):
        src = lax.rem(my_c + d, n_col)
        return pltpu.make_async_remote_copy(
            src_ref=rx_n.at[m, src], dst_ref=rx_n.at[m, src], send_sem=send_n.at[m, d], recv_sem=recv_n.at[m, src],
            device_id=(src, my_r), device_id_type=MESH)

    def wide_copy(m, d):
        peer = lax.rem(my_r + d, n_row)
        return pltpu.make_async_remote_copy(
            src_ref=rx_w.at[m, my_r], dst_ref=rx_w.at[m, my_r], send_sem=send_w.at[m, d], recv_sem=recv_w.at[m, my_r],
            device_id=(my_c, peer), device_id_type=MESH)

    def wide_arrival(m, d):
        src = lax.rem(my_r + d, n_row)
        return pltpu.make_async_remote_copy(
            src_ref=rx_w.at[m, src], dst_ref=rx_w.at[m, src], send_sem=send_w.at[m, d], recv_sem=recv_w.at[m, src],
            device_id=(my_c, src), device_id_type=MESH)

    def scalar_copy(m, d):
        peer = lax.rem(me + d, n_dev)
        return pltpu.make_async_remote_copy(
            src_ref=rx_s.at[m, me], dst_ref=rx_s.at[m, me], send_sem=send_s.at[m, d], recv_sem=recv_s.at[m, me],
            device_id=(peer // n_row, lax.rem(peer, n_row)), device_id_type=MESH)

    def scalar_arrival(m, d):
        src = lax.rem(me + d, n_dev)
        return pltpu.make_async_remote_copy(
            src_ref=rx_s.at[m, src], dst_ref=rx_s.at[m, src], send_sem=send_s.at[m, d], recv_sem=recv_s.at[m, src],
            device_id=(src // n_row, lax.rem(src, n_row)), device_id_type=MESH)

    def products(m):
        slot = lax.rem(m, 2)
        for copy in loads(m, slot)[0]:
            copy.wait()

        @pl.when(m + 1 < n_mat)
        def _():
            start_loads(m + 1, 1 - slot)

        for i in range(n_mat):
            @pl.when(m == i)
            def _():
                w_copies[i].start()

        total = jnp.zeros((8, narrow), F32)
        for s in range(0, wide, chunk):
            g = jnp.dot(b_buf[slot, s:s + chunk, :], a_buf[slot], preferred_element_type=F32)
            upd[m, s:s + chunk, :] = g
            q = g * g
            part = q[:, :LANES]
            for t, tw in nt[1:]:
                part = part + q[:, t:t + tw]
            row_acc[s:s + chunk, :] = part
            total = total + jnp.sum(q.reshape(chunk // 8, 8, narrow), axis=0)
        sums = jnp.sum(total, axis=0, keepdims=True)
        for j, (t, tw) in enumerate(nt):
            rx_n[m, my_c, j:j + 1, :] = sums[:, t:t + tw]
        for d in range(1, n_col):
            narrow_copy(m, d).start()
        for j, (t, tw) in enumerate(tiles):
            block = row_acc[t:t + tw, :].T
            rx_w[m, my_r, j:j + 1, :tw] = jnp.sum(block, axis=0, keepdims=True)
        for d in range(1, n_row):
            wide_copy(m, d).start()

    lane = lax.broadcasted_iota(jnp.int32, (1, LANES), 1)

    def second_moments(m):
        beta = hyper[0]
        layer = lax.rem(m, layers)
        is_in = m < layers
        for d in range(1, n_col):
            narrow_arrival(m, d).wait_recv()
        for d in range(1, n_row):
            wide_arrival(m, d).wait_recv()
        sum_n = rx_n[m, 0]
        for src in range(1, n_col):
            sum_n = sum_n + rx_n[m, src]
        sum_w = rx_w[m, 0]
        for src in range(1, n_row):
            sum_w = sum_w + rx_w[m, src]
        new_n = beta * old_n[m] + (1.0 - beta) * (sum_n / full_wide + EPS_ONE)
        new_w = beta * old_w[m] + (1.0 - beta) * (sum_w / full_narrow + EPS_ONE)
        new_narrow[m] = new_n
        new_wide[m] = new_w

        def block_mean(v, length):
            index = (lax.broadcasted_iota(jnp.int32, v.shape, 0) * LANES + lax.broadcasted_iota(jnp.int32, v.shape, 1))
            masked = jnp.where(index < length, v, 0.0)
            return jnp.sum(jnp.sum(masked, axis=0, keepdims=True), axis=1, keepdims=True) / length

        mean_row = jnp.where(is_in, block_mean(new_n, narrow), block_mean(new_w, wide))
        one = jnp.ones_like(mean_row)
        inv_n = lax.rsqrt(new_n / jnp.where(is_in, mean_row, one))
        inv_w = lax.rsqrt(new_w / jnp.where(is_in, one, mean_row))
        for j, (t, tw) in enumerate(tiles):
            w_col[t:t + tw, :] = jnp.broadcast_to(inv_w[j:j + 1, :tw], (LANES, tw)).T
        inv_rows = [jnp.broadcast_to(inv_n[j:j + 1, :], (8, LANES)) for j in range(len(nt))]

        def scale(i, acc):
            rows = pl.ds(pl.multiple_of(i * 8, 8), 8)
            a = w_col[rows, :]
            for j, (t, tw) in enumerate(nt):
                u = upd[m, rows, t:t + tw] * a * inv_rows[j]
                upd[m, rows, t:t + tw] = u
                acc = acc + u * u
            return acc

        total = jnp.sum(lax.fori_loop(0, wide // 8, scale, jnp.zeros((8, LANES), F32), unroll=6), keepdims=True)

        def send(wv):
            def square(i, acc):
                rows = pl.ds(pl.multiple_of(i * 8, 8), 8)
                for t, tw in nt:
                    v = wv[layer, rows, t:t + tw]
                    acc = acc + v * v
                return acc

            w_sq = jnp.sum(lax.fori_loop(0, wide // 8, square, jnp.zeros((8, LANES), F32), unroll=6), keepdims=True)
            rx_s[m, me] = jnp.where(lane < 32, total, jnp.where(lane < 64, w_sq, mean_row))

        on_weights(m, send)
        for d in range(1, n_dev):
            scalar_copy(m, d).start()

    def step_factor(m):
        for d in range(1, n_dev):
            scalar_arrival(m, d).wait_recv()
        got = [rx_s[m, src] for src in range(n_dev)]
        mean = got[0]
        for v in got[1:]:
            mean = mean + v
        s_full = jnp.sum(jnp.where(lane == 64, mean, 0.0), axis=1, keepdims=True) / n_dev
        own = jnp.sum(jnp.where(lane == 64, rx_s[m, me], 0.0), axis=1, keepdims=True)
        acc = None
        for v in got:
            ratio = s_full / pltpu.roll(v, 64, 1)
            term = v * jnp.where(lane < 32, ratio, 1.0)
            acc = term if acc is None else acc + term
        upd_sq = jnp.sum(jnp.where(lane == 0, acc, 0.0), axis=1, keepdims=True)
        w_sq = jnp.sum(jnp.where(lane == 32, acc, 0.0), axis=1, keepdims=True)
        upd_rms = jnp.sqrt(upd_sq / n_total)
        w_rms = jnp.sqrt(w_sq / n_total)
        size = hyper[1] * jnp.maximum(EPS_TWO, w_rms) / jnp.maximum(1.0, upd_rms / hyper[2])
        k = jnp.broadcast_to(size * jnp.sqrt(s_full / own), (8, LANES))
        layer = lax.rem(m, layers)

        def apply(wv):
            def update(i, carry):
                rows = pl.ds(pl.multiple_of(i * 8, 8), 8)
                for t, tw in nt:
                    wv[layer, rows, t:t + tw] = wv[layer, rows, t:t + tw] - k * upd[m, rows, t:t + tw]
                return carry
            lax.fori_loop(0, wide // 8, update, 0, unroll=6)

        on_weights(m, apply)

    def body(i, _):
        @pl.when(i < n_mat)
        def _():
            products(i)

        for m in range(n_mat):
            @pl.when(i == m + 1)
            def _(m=m):
                w_copies[m].wait()

        @pl.when(jnp.logical_and(i >= 1, i <= n_mat))
        def _():
            second_moments(i - 1)

        @pl.when(i >= 2)
        def _():
            step_factor(i - 2)
        return 0

    lax.fori_loop(0, n_mat + 2, body, 0)

    def drain(m, _):
        for d in range(1, n_col):
            narrow_copy(m, d).wait_send()
        for d in range(1, n_row):
            wide_copy(m, d).wait_send()
        for d in range(1, n_dev):
            scalar_copy(m, d).wait_send()
        return 0

    lax.fori_loop(0, n_mat, drain, 0)
    for layer in range(layers):
        for m, dst_n, dst_w in ((layer, row_in_new, col_in_new), (layers + layer, col_out_new, row_out_new)):
            for j, (s, w) in enumerate(nt):
                dst_n[layer:layer + 1, s:s + w] = new_narrow[m, j:j + 1, :w]
            for j, (s, w) in enumerate(tiles):
                dst_w[layer:layer + 1, s:s + w] = new_wide[m, j:j + 1, :w]


def write_kernel(*refs):
    count = (len(refs) - 1) // 2
    srcs, dsts, sem = refs[:count], refs[count:2 * count], refs[-1]
    copies = [pltpu.make_async_copy(src, dst, sem.at[i]) for i, (src, dst) in enumerate(zip(srcs, dsts))]
    for copy in copies:
        copy.start()
    for copy in copies:
        copy.wait()


def solution(mesh):
    n_col = mesh.shape['col']
    n_row = mesh.shape['row']
    tile_in = P(None, 'row', 'col')
    tile_out = P(None, 'col', 'row')
    lane_row = P(None, None, 'row')
    lane_col = P(None, None, 'col')
    vec_row = P(None, 'row')
    vec_col = P(None, 'col')

    def local_step(hyper_params, w_in, x_in, dy_in, row_in, col_in, w_out, x_out, dy_out, row_out, col_out):
        layers, narrow, wide = w_in.shape
        tokens = x_in.shape[1]
        n_mat = 2 * layers
        n_dev = n_col * n_row
        hbm = pl.BlockSpec(memory_space=pltpu.HBM)
        vmem = pl.BlockSpec(memory_space=pltpu.VMEM)
        smem = pl.BlockSpec(memory_space=pltpu.SMEM)
        dma = pltpu.SemaphoreType.DMA
        nr, wr = 8, 16
        swap = lambda v: jnp.swapaxes(v, 1, 2)
        chunk = 336
        shapes = [v.shape for v in (w_out, row_in, col_in, w_out, row_out, col_out)]
        results = pl.pallas_call(
            functools.partial(stats_kernel, n_col, n_row, chunk),
            out_shape=tuple(pltpu.VMEM(shape, F32) for shape in shapes),
            in_specs=[smem, hbm, hbm, hbm, vmem, vmem, hbm, hbm, hbm, vmem, vmem],
            out_specs=(vmem,) * 6,
            scratch_shapes=[
                pltpu.VMEM((n_mat, wide, narrow), F32),
                pltpu.VMEM((2, tokens, narrow), jnp.bfloat16),
                pltpu.VMEM((2, wide, tokens), jnp.bfloat16),
                pltpu.VMEM((wide, LANES), F32),
                pltpu.VMEM((8, narrow), F32),
                pltpu.VMEM((wide, LANES), F32),
                pltpu.VMEM((n_mat, n_col, nr, LANES), F32),
                pltpu.VMEM((n_mat, n_row, wr, LANES), F32),
                pltpu.VMEM((n_mat, n_dev, 1, LANES), F32),
                pltpu.VMEM((n_mat, nr, LANES), F32),
                pltpu.VMEM((n_mat, wr, LANES), F32),
                pltpu.VMEM((n_mat, nr, LANES), F32),
                pltpu.VMEM((n_mat, wr, LANES), F32),
                dma((2,)), dma((2,)), dma((n_mat,)),
                dma((n_mat, n_col)), dma((n_mat, n_col)),
                dma((n_mat, n_row)), dma((n_mat, n_row)),
                dma((n_mat, n_dev)), dma((n_mat, n_dev)),
            ],
            compiler_params=pltpu.CompilerParams(collective_id=0, has_side_effects=True, vmem_limit_bytes=44 << 20),
            name="stats",
        )(hyper_params, swap(w_in), x_in, swap(dy_in), row_in, col_in, w_out, swap(x_out), dy_out, row_out, col_out)
        w_in_new, row_in_new, col_in_new, w_out_new, row_out_new, col_out_new = pl.pallas_call(
            write_kernel,
            out_shape=tuple(pltpu.HBM(shape, F32) for shape in shapes),
            in_specs=[vmem] * 6,
            out_specs=(hbm,) * 6,
            scratch_shapes=[dma((6,))],
            compiler_params=pltpu.CompilerParams(vmem_limit_bytes=1 << 20),
            name="write",
        )(*(pltpu.with_memory_space_constraint(v, pltpu.VMEM) for v in results))
        return swap(w_in_new), row_in_new, col_in_new, w_out_new, row_out_new, col_out_new

    return jax.shard_map(local_step, mesh=mesh, in_specs=(P(), tile_in, lane_row, lane_col, vec_row, vec_col, tile_out, lane_col, lane_row, vec_col, vec_row), out_specs=(tile_in, vec_row, vec_col, tile_out, vec_col, vec_row), check_vma=False)
```

profile of v0, /device:TPU:0, one launch (start us, length us, event | category | flops | bytes accessed | tf_op | source)
XLA Modules:
  0.0 61.2 jit_solution(11446148747355318983)
XLA Ops:
  0.6 54.2 %stats.1 = (f32[2,1680,640]{2,1,0:T(8,128)S(1)}, f32[2,640]{1,0:T(2,128)S(1)}, f32[2,1680]{1,0:T(2,128)S(1)}, f32[2,1680,640]{2,1,0:T(8,128)S(1)}, f32[2,1680]{1,0:T(2,128)S(1)}, /*index=5*/f32[2,640]{1,0:T(2,128)S(1)}) custom-call(f32[3]{0:T(128)} %hyper.1, f32[2,1680,640]{2,1,0:T(8,128)} %bitcast.6, bf16[2,2048,640]{2,1,0:T(8,128)(2,1)} %x_in.1, ...), custom_call_target="tpu_custom_call" | custom-call | tf_op jit(solution)/shard_map/stats/pallas_call | solution.py:322
  54.8 6.4 %write.1 = (f32[2,1680,640]{2,1,0:T(8,128)}, f32[2,640]{1,0:T(2,128)}, f32[2,1680]{1,0:T(2,128)}, f32[2,1680,640]{2,1,0:T(8,128)}, f32[2,1680]{1,0:T(2,128)}, /*index=5*/f32[2,640]{1,0:T(2,128)}) custom-call(f32[2,1680,640]{2,1,0:T(8,128)S(1)} %get-tuple-element.18.refs_0_, f32[2,640]{1,0:T(2,128)S(1)} %get-tuple-element.19.refs_1_, ...), custom_call_target="tpu_custom_call" | custom-call | tf_op jit(solution)/shard_map/write/pallas_call | solution.py:349
where the time goes:
time: 61.4 us; the launch traced here: 61.2 us
  Pallas kernels  60.5 us (99%)
  between operations  0.64 us (1%)
    pallas_call x1, Pallas kernels, local_step(): pl.pallas_call(functools.partial(stats_kernel, n_col, n_row, chunk), out_...  54.2 us
    pallas_call x1, Pallas kernels, local_step(): pl.pallas_call(write_kernel, out_shape=tuple((pltpu.HBM(shape, F32) for s...  6.37 us

commit v1 on v0

v1 whole, which is shorter than its diff:
```python
import functools

import jax
import jax.numpy as jnp
from jax import lax
from jax.experimental import pallas as pl
from jax.experimental.pallas import tpu as pltpu
from jax.sharding import PartitionSpec as P

EPS_ONE = 1e-30
EPS_TWO = 1e-3
MESH = pl.DeviceIdType.MESH
F32 = jnp.float32
LANES = 128


def col_tiles(width):
    return [(start, min(LANES, width - start)) for start in range(0, width, LANES)]


def stats_kernel(n_col, n_row, chunk, hyper, w_in, x_in, dy_in, row_in, col_in, w_out, x_out, dy_out, row_out, col_out,
                 wv_in, row_in_new, col_in_new, wv_out, row_out_new, col_out_new,
                 upd, a_buf, b_buf, row_acc, w_col, inv_n, rx_n, rx_w, rx_s, old_n, old_w,
                 a_sem, b_sem, w_sem, send_n, recv_n, send_w, recv_w, send_s, recv_s):
    n_mat, wide, narrow = upd.shape
    layers = n_mat // 2
    full_narrow, full_wide = narrow * n_row, wide * n_col
    n_total = float(full_narrow * full_wide)
    my_c, my_r = lax.axis_index("col"), lax.axis_index("row")
    n_dev = n_col * n_row
    me = my_c * n_row + my_r
    tiles = col_tiles(wide)
    nt = col_tiles(narrow)

    order = [(s, chunk) for s in range(0, wide, chunk)]

    def loads(m):
        slot, layer = m % 2, m % layers
        a_src, b_src = (x_in, dy_in) if m < layers else (dy_out, x_out)
        return ([pltpu.make_async_copy(a_src.at[layer], a_buf.at[slot], a_sem.at[slot])]
                + [pltpu.make_async_copy(b_src.at[layer, pl.ds(s, w)], b_buf.at[slot, pl.ds(s, w)], b_sem.at[slot, i])
                   for i, (s, w) in enumerate(order)])

    for copy in loads(0):
        copy.start()
    barrier = pltpu.get_barrier_semaphore()
    for d in range(1, n_dev):
        peer = lax.rem(me + d, n_dev)
        pl.semaphore_signal(barrier, inc=1, device_id=(peer // n_row, lax.rem(peer, n_row)), device_id_type=MESH)

    old_n[...] = jnp.zeros_like(old_n)
    old_w[...] = jnp.zeros_like(old_w)
    for m in range(n_mat):
        rx_n[m, my_c] = jnp.zeros(rx_n.shape[2:], F32)
        rx_w[m, my_r] = jnp.zeros(rx_w.shape[2:], F32)
    for layer in range(layers):
        for m, src_n, src_w in ((layer, row_in, col_in), (layers + layer, col_out, row_out)):
            for j, (s, w) in enumerate(nt):
                old_n[m, j:j + 1, :w] = src_n[layer:layer + 1, s:s + w]
            for j, (s, w) in enumerate(tiles):
                old_w[m, j:j + 1, :w] = src_w[layer:layer + 1, s:s + w]

    w_copies = ([pltpu.make_async_copy(w_in.at[i], wv_in.at[i], w_sem.at[i]) for i in range(layers)]
                + [pltpu.make_async_copy(w_out.at[i], wv_out.at[i], w_sem.at[layers + i]) for i in range(layers)])

    def weights(m):
        return wv_in.at[m % layers] if m < layers else wv_out.at[m % layers]

    def narrow_copy(m, d):
        peer = lax.rem(my_c + d, n_col)
        return pltpu.make_async_remote_copy(
            src_ref=rx_n.at[m, my_c], dst_ref=rx_n.at[m, my_c], send_sem=send_n.at[m, d], recv_sem=recv_n.at[m, my_c],
            device_id=(peer, my_r), device_id_type=MESH)

    def narrow_arrival(m, d):
        src = lax.rem(my_c + d, n_col)
        return pltpu.make_async_remote_copy(
            src_ref=rx_n.at[m, src], dst_ref=rx_n.at[m, src], send_sem=send_n.at[m, d], recv_sem=recv_n.at[m, src],
            device_id=(src, my_r), device_id_type=MESH)

    def wide_copy(m, d):
        peer = lax.rem(my_r + d, n_row)
        return pltpu.make_async_remote_copy(
            src_ref=rx_w.at[m, my_r], dst_ref=rx_w.at[m, my_r], send_sem=send_w.at[m, d], recv_sem=recv_w.at[m, my_r],
            device_id=(my_c, peer), device_id_type=MESH)

    def wide_arrival(m, d):
        src = lax.rem(my_r + d, n_row)
        return pltpu.make_async_remote_copy(
            src_ref=rx_w.at[m, src], dst_ref=rx_w.at[m, src], send_sem=send_w.at[m, d], recv_sem=recv_w.at[m, src],
            device_id=(my_c, src), device_id_type=MESH)

    def scalar_copy(m, d):
        peer = lax.rem(me + d, n_dev)
        return pltpu.make_async_remote_copy(
            src_ref=rx_s.at[m, me], dst_ref=rx_s.at[m, me], send_sem=send_s.at[m, d], recv_sem=recv_s.at[m, me],
            device_id=(peer // n_row, lax.rem(peer, n_row)), device_id_type=MESH)

    def scalar_arrival(m, d):
        src = lax.rem(me + d, n_dev)
        return pltpu.make_async_remote_copy(
            src_ref=rx_s.at[m, src], dst_ref=rx_s.at[m, src], send_sem=send_s.at[m, d], recv_sem=recv_s.at[m, src],
            device_id=(src // n_row, lax.rem(src, n_row)), device_id_type=MESH)

    lane = lax.broadcasted_iota(jnp.int32, (1, LANES), 1)
    zero = jnp.zeros((8, LANES), F32)
    sq_sum = {}
    norm_sum = {}
    row_mean = {}

    def fold(v):
        return jnp.sum(v.reshape(v.shape[0] // 8, 8, v.shape[1]), axis=0)

    def scale_rows(m, s, w):
        acc = norm_sum.get(m, zero)
        a = w_col[m % 2, s:s + w, :]
        for j, (t, tw) in enumerate(nt):
            u = upd[m, s:s + w, t:t + tw] * a * inv_n[m, j:j + 1, :]
            upd[m, s:s + w, t:t + tw] = u
            acc = acc + fold(u * u)
        norm_sum[m] = acc

    def square_rows(m, s, w):
        acc = sq_sum.get(m, zero)
        for t, tw in nt:
            v = weights(m)[s:s + w, t:t + tw]
            acc = acc + fold(v * v)
        sq_sum[m] = acc

    def products(m, blocks, total, beside):
        slot = m % 2
        for s, w in blocks:
            g = jnp.dot(b_buf[slot, s:s + w, :], a_buf[slot], preferred_element_type=F32)
            upd[m, s:s + w, :] = g
            q = g * g
            part = q[:, :LANES]
            for t, tw in nt[1:]:
                part = part + q[:, t:t + tw]
            total = total + fold(q)
            row_acc[s:s + w, :] = part
            for t, tw in tiles:
                if s < t + tw <= s + w:
                    block = row_acc[t:t + tw, :].T
                    j = t // LANES
                    rx_w[m, my_r, j:j + 1, :tw] = jnp.sum(block, axis=0, keepdims=True)
            for fn in beside:
                fn(s, w)
        return total

    def send_moments(m, total):
        sums = jnp.sum(total, axis=0, keepdims=True)
        for j, (t, tw) in enumerate(nt):
            rx_n[m, my_c, j:j + 1, :] = sums[:, t:t + tw]
        for d in range(1, n_col):
            narrow_copy(m, d).start()
        for d in range(1, n_row):
            wide_copy(m, d).start()

    def wait_moments(m):
        for d in range(1, n_col):
            narrow_arrival(m, d).wait_recv()
        for d in range(1, n_row):
            wide_arrival(m, d).wait_recv()

    def second_moments(m):
        beta = hyper[0]
        layer = m % layers
        sum_n = rx_n[m, 0]
        for src in range(1, n_col):
            sum_n = sum_n + rx_n[m, src]
        sum_w = rx_w[m, 0]
        for src in range(1, n_row):
            sum_w = sum_w + rx_w[m, src]
        new_n = beta * old_n[m] + (1.0 - beta) * (sum_n / full_wide + EPS_ONE)
        new_w = beta * old_w[m] + (1.0 - beta) * (sum_w / full_narrow + EPS_ONE)
        dst_n, dst_w = (row_in_new, col_in_new) if m < layers else (col_out_new, row_out_new)
        for j, (t, tw) in enumerate(nt):
            dst_n[layer:layer + 1, t:t + tw] = new_n[j:j + 1, :tw]
        for j, (t, tw) in enumerate(tiles):
            dst_w[layer:layer + 1, t:t + tw] = new_w[j:j + 1, :tw]
        v, length = (new_n, narrow) if m < layers else (new_w, wide)
        index = lax.broadcasted_iota(jnp.int32, v.shape, 0) * LANES + lax.broadcasted_iota(jnp.int32, v.shape, 1)
        mean = jnp.sum(jnp.sum(jnp.where(index < length, v, 0.0), axis=0, keepdims=True), axis=1, keepdims=True) / length
        row_mean[m] = mean
        scaled_n, scaled_w = (new_n / mean, new_w) if m < layers else (new_n, new_w / mean)
        inv_n[m] = lax.rsqrt(scaled_n)
        inv_w = lax.rsqrt(scaled_w)
        for j, (t, tw) in enumerate(tiles):
            w_col[m % 2, t:t + tw, :] = jnp.broadcast_to(inv_w[j:j + 1, :tw], (LANES, tw)).T

    def each_peer(fn):
        def body(d, carry):
            fn(d)
            return carry
        lax.fori_loop(1, n_dev, body, 0)

    def send_scalars(m):
        norm = jnp.sum(norm_sum[m], keepdims=True)
        w_sq = jnp.sum(sq_sum[m], keepdims=True)
        rx_s[m, me] = jnp.where(lane < 32, norm, jnp.where(lane < 64, w_sq, row_mean[m]))
        each_peer(lambda d: scalar_copy(m, d).start())

    def step_factor(m):
        each_peer(lambda d: scalar_arrival(m, d).wait_recv())
        got = rx_s[m]
        s_full = jnp.sum(jnp.where(lane == 64, jnp.sum(got, axis=0), 0.0), axis=1, keepdims=True) / n_dev
        own = jnp.sum(jnp.where(lane == 64, rx_s[m, me], 0.0), axis=1, keepdims=True)
        ratio = s_full[None] / pltpu.roll(got, 64, 2)
        acc = jnp.sum(got * jnp.where(lane[None] < 32, ratio, 1.0), axis=0)
        upd_sq = jnp.sum(jnp.where(lane == 0, acc, 0.0), axis=1, keepdims=True)
        w_sq = jnp.sum(jnp.where(lane == 32, acc, 0.0), axis=1, keepdims=True)
        upd_rms = jnp.sqrt(upd_sq / n_total)
        w_rms = jnp.sqrt(w_sq / n_total)
        size = hyper[1] * jnp.maximum(EPS_TWO, w_rms) / jnp.maximum(1.0, upd_rms / hyper[2])
        return jnp.broadcast_to(size * jnp.sqrt(s_full / own), (8, LANES))

    def update(m):
        k = step_factor(m)
        w_ref = weights(m)

        def body(i, carry):
            rows = pl.ds(pl.multiple_of(i * 8, 8), 8)
            for t, tw in nt:
                w_ref[rows, t:t + tw] = w_ref[rows, t:t + tw] - k * upd[m, rows, t:t + tw]
            return carry
        lax.fori_loop(0, wide // 8, body, 0, unroll=6)

    last = n_mat - 1
    for m in range(n_mat):
        total = jnp.zeros((8, narrow), F32)
        copies = loads(m)
        blocks = order
        if m == 0:
            for copy in copies[:2]:
                copy.wait()
            for copy in loads(1):
                copy.start()
            total = products(m, order[:1], total, [])
            blocks, copies = order[1:], copies[2:]
        for copy in copies:
            copy.wait()
        if 1 <= m < last:
            for copy in loads(m + 1):
                copy.start()
        w_copies[m].start()
        beside = []
        if m >= 1:
            w_copies[m - 1].wait()
            beside.append(functools.partial(square_rows, m - 1))
        if m >= 2:
            wait_moments(m - 2)
            second_moments(m - 2)
            beside.append(functools.partial(scale_rows, m - 2))
        total = products(m, blocks, total, beside)
        if m == 0:
            pl.semaphore_wait(barrier, n_dev - 1)
        send_moments(m, total)
        if m >= 2:
            send_scalars(m - 2)

    w_copies[last].wait()
    wait_moments(last - 1)
    second_moments(last - 1)
    for s, w in order:
        scale_rows(last - 1, s, w)
    send_scalars(last - 1)
    for s, w in order:
        square_rows(last, s, w)
    for m in range(last - 2):
        update(m)
    wait_moments(last)
    second_moments(last)
    for s, w in order:
        scale_rows(last, s, w)
    send_scalars(last)
    for m in range(last - 2, last):
        update(m)
    update(last)

    def drain(m, _):
        for d in range(1, n_col):
            narrow_copy(m, d).wait_send()
        for d in range(1, n_row):
            wide_copy(m, d).wait_send()
        for d in range(1, n_dev):
            scalar_copy(m, d).wait_send()
        return 0

    lax.fori_loop(0, n_mat, drain, 0)


def write_kernel(*refs):
    count = (len(refs) - 1) // 2
    srcs, dsts, sem = refs[:count], refs[count:2 * count], refs[-1]
    copies = [pltpu.make_async_copy(src, dst, sem.at[i]) for i, (src, dst) in enumerate(zip(srcs, dsts))]
    for copy in copies:
        copy.start()
    for copy in copies:
        copy.wait()


def solution(mesh):
    n_col = mesh.shape['col']
    n_row = mesh.shape['row']
    tile_in = P(None, 'row', 'col')
    tile_out = P(None, 'col', 'row')
    lane_row = P(None, None, 'row')
    lane_col = P(None, None, 'col')
    vec_row = P(None, 'row')
    vec_col = P(None, 'col')

    def local_step(hyper_params, w_in, x_in, dy_in, row_in, col_in, w_out, x_out, dy_out, row_out, col_out):
        layers, narrow, wide = w_in.shape
        tokens = x_in.shape[1]
        n_mat = 2 * layers
        n_dev = n_col * n_row
        hbm = pl.BlockSpec(memory_space=pltpu.HBM)
        vmem = pl.BlockSpec(memory_space=pltpu.VMEM)
        smem = pl.BlockSpec(memory_space=pltpu.SMEM)
        dma = pltpu.SemaphoreType.DMA
        nr, wr = 8, 16
        swap = lambda v: jnp.swapaxes(v, 1, 2)
        chunk = 336
        shapes = [v.shape for v in (w_out, row_in, col_in, w_out, row_out, col_out)]
        results = pl.pallas_call(
            functools.partial(stats_kernel, n_col, n_row, chunk),
            out_shape=tuple(pltpu.VMEM(shape, F32) for shape in shapes),
            in_specs=[smem, hbm, hbm, hbm, vmem, vmem, hbm, hbm, hbm, vmem, vmem],
            out_specs=(vmem,) * 6,
            scratch_shapes=[
                pltpu.VMEM((n_mat, wide, narrow), F32),
                pltpu.VMEM((2, tokens, narrow), jnp.bfloat16),
                pltpu.VMEM((2, wide, tokens), jnp.bfloat16),
                pltpu.VMEM((wide, LANES), F32),
                pltpu.VMEM((2, wide, LANES), F32),
                pltpu.VMEM((n_mat, nr, LANES), F32),
                pltpu.VMEM((n_mat, n_col, nr, LANES), F32),
                pltpu.VMEM((n_mat, n_row, wr, LANES), F32),
                pltpu.VMEM((n_mat, n_dev, 1, LANES), F32),
                pltpu.VMEM((n_mat, nr, LANES), F32),
                pltpu.VMEM((n_mat, wr, LANES), F32),
                dma((2,)), dma((2, wide // chunk)), dma((n_mat,)),
                dma((n_mat, n_col)), dma((n_mat, n_col)),
                dma((n_mat, n_row)), dma((n_mat, n_row)),
                dma((n_mat, n_dev)), dma((n_mat, n_dev)),
            ],
            compiler_params=pltpu.CompilerParams(collective_id=0, has_side_effects=True, vmem_limit_bytes=44 << 20),
            name="stats",
        )(hyper_params, swap(w_in), x_in, swap(dy_in), row_in, col_in, w_out, swap(x_out), dy_out, row_out, col_out)
        w_in_new, row_in_new, col_in_new, w_out_new, row_out_new, col_out_new = pl.pallas_call(
            write_kernel,
            out_shape=tuple(pltpu.HBM(shape, F32) for shape in shapes),
            in_specs=[vmem] * 6,
            out_specs=(hbm,) * 6,
            scratch_shapes=[dma((6,))],
            compiler_params=pltpu.CompilerParams(vmem_limit_bytes=1 << 20),
            name="write",
        )(*(pltpu.with_memory_space_constraint(v, pltpu.VMEM) for v in results))
        return swap(w_in_new), row_in_new, col_in_new, w_out_new, row_out_new, col_out_new

    return jax.shard_map(local_step, mesh=mesh, in_specs=(P(), tile_in, lane_row, lane_col, vec_row, vec_col, tile_out, lane_col, lane_row, vec_col, vec_row), out_specs=(tile_in, vec_row, vec_col, tile_out, vec_col, vec_row), check_vma=False)
```

time: 61.4 us -> 52.8 us (0.86)
  Pallas kernels: 60.5 us -> 51.8 us
    pallas_call x1, Pallas kernels: 54.2 us -> 45.4 us  [local_step(): pl.pallas_call(functools.partial(stats_kernel, n_col, n_row, chunk), out_...]
where the time goes in v1:
time: 52.8 us; the launch traced here: 52.6 us
  Pallas kernels  51.8 us (98%)
  between operations  0.8 us (2%)
    pallas_call x1, Pallas kernels, local_step(): pl.pallas_call(functools.partial(stats_kernel, n_col, n_row, chunk), out_...  45.4 us
    pallas_call x1, Pallas kernels, local_step(): pl.pallas_call(write_kernel, out_shape=tuple((pltpu.HBM(shape, F32) for s...  6.37 us

profile of v1, /device:TPU:0, one launch (start us, length us, event | category | flops | bytes accessed | tf_op | source)
XLA Modules:
  0.0 52.6 jit_solution(15867401772830900026)
XLA Ops:
  0.6 45.4 %stats.1 = (f32[2,1680,640]{2,1,0:T(8,128)S(1)}, f32[2,640]{1,0:T(2,128)S(1)}, f32[2,1680]{1,0:T(2,128)S(1)}, f32[2,1680,640]{2,1,0:T(8,128)S(1)}, f32[2,1680]{1,0:T(2,128)S(1)}, /*index=5*/f32[2,640]{1,0:T(2,128)S(1)}) custom-call(f32[3]{0:T(128)} %hyper.1, f32[2,1680,640]{2,1,0:T(8,128)} %bitcast.6, bf16[2,2048,640]{2,1,0:T(8,128)(2,1)} %x_in.1, ...), custom_call_target="tpu_custom_call" | custom-call | tf_op jit(solution)/shard_map/stats/pallas_call | solution.py:325
  46.1 6.4 %write.1 = (f32[2,1680,640]{2,1,0:T(8,128)}, f32[2,640]{1,0:T(2,128)}, f32[2,1680]{1,0:T(2,128)}, f32[2,1680,640]{2,1,0:T(8,128)}, f32[2,1680]{1,0:T(2,128)}, /*index=5*/f32[2,640]{1,0:T(2,128)}) custom-call(f32[2,1680,640]{2,1,0:T(8,128)S(1)} %get-tuple-element.18.refs_0_, f32[2,640]{1,0:T(2,128)S(1)} %get-tuple-element.19.refs_1_, ...), custom_call_target="tpu_custom_call" | custom-call | tf_op jit(solution)/shard_map/write/pallas_call | solution.py:350

commit v2 on v1

--- a/solution.py
+++ b/solution.py
@@ -18,7 +18,7 @@
     return [(start, min(LANES, width - start)) for start in range(0, width, LANES)]
 
 
-def stats_kernel(n_col, n_row, chunk, hyper, w_in, x_in, dy_in, row_in, col_in, w_out, x_out, dy_out, row_out, col_out,
+def stats_kernel(n_col, n_row, sizes, hyper, w_in, x_in, dy_in, row_in, col_in, w_out, x_out, dy_out, row_out, col_out,
                  wv_in, row_in_new, col_in_new, wv_out, row_out_new, col_out_new,
                  upd, a_buf, b_buf, row_acc, w_col, inv_n, rx_n, rx_w, rx_s, old_n, old_w,
                  a_sem, b_sem, w_sem, send_n, recv_n, send_w, recv_w, send_s, recv_s):
@@ -32,7 +32,10 @@
     tiles = col_tiles(wide)
     nt = col_tiles(narrow)
 
-    order = [(s, chunk) for s in range(0, wide, chunk)]
+    def split(start, *lengths):
+        return [(start + sum(lengths[:i]), w) for i, w in enumerate(lengths)]
+
+    order = split(0, *sizes)
 
     def loads(m):
         slot, layer = m % 2, m % layers
@@ -103,31 +106,31 @@
             device_id=(src // n_row, lax.rem(src, n_row)), device_id_type=MESH)
 
     lane = lax.broadcasted_iota(jnp.int32, (1, LANES), 1)
-    zero = jnp.zeros((8, LANES), F32)
+    zero = jnp.zeros((8, narrow), F32)
     sq_sum = {}
     norm_sum = {}
     row_mean = {}
 
+    group = 16
+
     def fold(v):
-        return jnp.sum(v.reshape(v.shape[0] // 8, 8, v.shape[1]), axis=0)
-
-    def scale_rows(m, s, w):
-        acc = norm_sum.get(m, zero)
-        a = w_col[m % 2, s:s + w, :]
-        for j, (t, tw) in enumerate(nt):
-            u = upd[m, s:s + w, t:t + tw] * a * inv_n[m, j:j + 1, :]
-            upd[m, s:s + w, t:t + tw] = u
-            acc = acc + fold(u * u)
-        norm_sum[m] = acc
-
-    def square_rows(m, s, w):
-        acc = sq_sum.get(m, zero)
-        for t, tw in nt:
-            v = weights(m)[s:s + w, t:t + tw]
-            acc = acc + fold(v * v)
-        sq_sum[m] = acc
-
-    def products(m, blocks, total, beside):
+        return sum(v[r:r + 8] for r in range(8, v.shape[0], 8)) + v[:8]
+
+    def scale_group(m, rows, acc):
+        a = jnp.concatenate([w_col[m % 2, rows, :]] * len(nt), axis=1)
+        u = upd[m, rows, :] * a * inv_n[m % 2]
+        upd[m, rows, :] = u
+        return acc + fold(u * u)
+
+    def square_group(m, rows, acc):
+        v = weights(m)[rows, :]
+        return acc + fold(v * v)
+
+    def all_rows(fn, sums, m):
+        sums[m] = lax.fori_loop(0, wide // group, lambda i, acc: fn(m, pl.ds(pl.multiple_of(i * group, group), group), acc),
+                                zero, unroll=5)
+
+    def products(m, blocks, total):
         slot = m % 2
         for s, w in blocks:
             g = jnp.dot(b_buf[slot, s:s + w, :], a_buf[slot], preferred_element_type=F32)
@@ -136,15 +139,13 @@
             part = q[:, :LANES]
             for t, tw in nt[1:]:
                 part = part + q[:, t:t + tw]
-            total = total + fold(q)
+            total = total + jnp.sum(q.reshape(w // 8, 8, narrow), axis=0)
             row_acc[s:s + w, :] = part
             for t, tw in tiles:
                 if s < t + tw <= s + w:
                     block = row_acc[t:t + tw, :].T
                     j = t // LANES
                     rx_w[m, my_r, j:j + 1, :tw] = jnp.sum(block, axis=0, keepdims=True)
-            for fn in beside:
-                fn(s, w)
         return total
 
     def send_moments(m, total):
@@ -182,9 +183,11 @@
         index = lax.broadcasted_iota(jnp.int32, v.shape, 0) * LANES + lax.broadcasted_iota(jnp.int32, v.shape, 1)
         mean = jnp.sum(jnp.sum(jnp.where(index < length, v, 0.0), axis=0, keepdims=True), axis=1, keepdims=True) / length
         row_mean[m] = mean
-        scaled_n, scaled_w = (new_n / mean, new_w) if m < layers else (new_n, new_w / mean)
-        inv_n[m] = lax.rsqrt(scaled_n)
-        inv_w = lax.rsqrt(scaled_w)
+        root = jnp.sqrt(mean)
+        scaled = lax.rsqrt(new_n) * root
+        for j, (t, tw) in enumerate(nt):
+            inv_n[m % 2, :, t:t + tw] = scaled[j:j + 1, :]
+        inv_w = lax.rsqrt(new_w)
         for j, (t, tw) in enumerate(tiles):
             w_col[m % 2, t:t + tw, :] = jnp.broadcast_to(inv_w[j:j + 1, :tw], (LANES, tw)).T
 
@@ -212,22 +215,21 @@
         upd_rms = jnp.sqrt(upd_sq / n_total)
         w_rms = jnp.sqrt(w_sq / n_total)
         size = hyper[1] * jnp.maximum(EPS_TWO, w_rms) / jnp.maximum(1.0, upd_rms / hyper[2])
-        return jnp.broadcast_to(size * jnp.sqrt(s_full / own), (8, LANES))
+        return size * jnp.sqrt(s_full / own)
 
     def update(m):
         k = step_factor(m)
         w_ref = weights(m)
 
         def body(i, carry):
-            rows = pl.ds(pl.multiple_of(i * 8, 8), 8)
-            for t, tw in nt:
-                w_ref[rows, t:t + tw] = w_ref[rows, t:t + tw] - k * upd[m, rows, t:t + tw]
+            rows = pl.ds(pl.multiple_of(i * group, group), group)
+            w_ref[rows, :] = w_ref[rows, :] - k * upd[m, rows, :]
             return carry
-        lax.fori_loop(0, wide // 8, body, 0, unroll=6)
+        lax.fori_loop(0, wide // group, body, 0, unroll=5)
 
     last = n_mat - 1
     for m in range(n_mat):
-        total = jnp.zeros((8, narrow), F32)
+        total = zero
         copies = loads(m)
         blocks = order
         if m == 0:
@@ -235,47 +237,29 @@
                 copy.wait()
             for copy in loads(1):
                 copy.start()
-            total = products(m, order[:1], total, [])
-            blocks, copies = order[1:], copies[2:]
+            total = products(m, split(0, 208, 224), total)
+            blocks, copies = order[1:-1] + split(order[-1][0], 208, 208), copies[2:]
         for copy in copies:
             copy.wait()
         if 1 <= m < last:
             for copy in loads(m + 1):
                 copy.start()
         w_copies[m].start()
-        beside = []
-        if m >= 1:
-            w_copies[m - 1].wait()
-            beside.append(functools.partial(square_rows, m - 1))
-        if m >= 2:
-            wait_moments(m - 2)
-            second_moments(m - 2)
-            beside.append(functools.partial(scale_rows, m - 2))
-        total = products(m, blocks, total, beside)
+        total = products(m, blocks, total)
         if m == 0:
             pl.semaphore_wait(barrier, n_dev - 1)
         send_moments(m, total)
-        if m >= 2:
-            send_scalars(m - 2)
-
-    w_copies[last].wait()
-    wait_moments(last - 1)
-    second_moments(last - 1)
-    for s, w in order:
-        scale_rows(last - 1, s, w)
-    send_scalars(last - 1)
-    for s, w in order:
-        square_rows(last, s, w)
-    for m in range(last - 2):
+
+    for m in range(n_mat):
+        w_copies[m].wait()
+        all_rows(square_group, sq_sum, m)
+    for m in range(n_mat):
+        wait_moments(m)
+        second_moments(m)
+        all_rows(scale_group, norm_sum, m)
+        send_scalars(m)
+    for m in range(n_mat):
         update(m)
-    wait_moments(last)
-    second_moments(last)
-    for s, w in order:
-        scale_rows(last, s, w)
-    send_scalars(last)
-    for m in range(last - 2, last):
-        update(m)
-    update(last)
 
     def drain(m, _):
         for d in range(1, n_col):
@@ -320,10 +304,10 @@
         dma = pltpu.SemaphoreType.DMA
         nr, wr = 8, 16
         swap = lambda v: jnp.swapaxes(v, 1, 2)
-        chunk = 336
+        sizes = (432, 416, 416, 416)
         shapes = [v.shape for v in (w_out, row_in, col_in, w_out, row_out, col_out)]
         results = pl.pallas_call(
-            functools.partial(stats_kernel, n_col, n_row, chunk),
+            functools.partial(stats_kernel, n_col, n_row, sizes),
             out_shape=tuple(pltpu.VMEM(shape, F32) for shape in shapes),
             in_specs=[smem, hbm, hbm, hbm, vmem, vmem, hbm, hbm, hbm, vmem, vmem],
             out_specs=(vmem,) * 6,
@@ -333,13 +317,13 @@
                 pltpu.VMEM((2, wide, tokens), jnp.bfloat16),
                 pltpu.VMEM((wide, LANES), F32),
                 pltpu.VMEM((2, wide, LANES), F32),
-                pltpu.VMEM((n_mat, nr, LANES), F32),
+                pltpu.VMEM((2, 1, narrow), F32),
                 pltpu.VMEM((n_mat, n_col, nr, LANES), F32),
                 pltpu.VMEM((n_mat, n_row, wr, LANES), F32),
                 pltpu.VMEM((n_mat, n_dev, 1, LANES), F32),
                 pltpu.VMEM((n_mat, nr, LANES), F32),
                 pltpu.VMEM((n_mat, wr, LANES), F32),
-                dma((2,)), dma((2, wide // chunk)), dma((n_mat,)),
+                dma((2,)), dma((2, len(sizes))), dma((n_mat,)),
                 dma((n_mat, n_col)), dma((n_mat, n_col)),
                 dma((n_mat, n_row)), dma((n_mat, n_row)),
                 dma((n_mat, n_dev)), dma((n_mat, n_dev)),

time: 52.8 us -> 52.1 us (0.987)
  Pallas kernels: 51.8 us -> 51.1 us
    pallas_call x1, Pallas kernels: 45.4 us -> 44.7 us  [local_step(): pl.pallas_call(functools.partial(stats_kernel, n_col, n_row, sizes), out_...]
where the time goes in v2:
time: 52.1 us; the launch traced here: 51.9 us
  Pallas kernels  51.1 us (98%)
  between operations  0.8 us (2%)
    pallas_call x1, Pallas kernels, local_step(): pl.pallas_call(functools.partial(stats_kernel, n_col, n_row, sizes), out_...  44.7 us
    pallas_call x1, Pallas kernels, local_step(): pl.pallas_call(write_kernel, out_shape=tuple((pltpu.HBM(shape, F32) for s...  6.37 us

profile of v2, /device:TPU:0, one launch (start us, length us, event | category | flops | bytes accessed | tf_op | source)
XLA Modules:
  0.0 51.9 jit_solution(2283752381640646088)
XLA Ops:
  0.6 44.7 %stats.1 = (f32[2,1680,640]{2,1,0:T(8,128)S(1)}, f32[2,640]{1,0:T(2,128)S(1)}, f32[2,1680]{1,0:T(2,128)S(1)}, f32[2,1680,640]{2,1,0:T(8,128)S(1)}, f32[2,1680]{1,0:T(2,128)S(1)}, /*index=5*/f32[2,640]{1,0:T(2,128)S(1)}) custom-call(f32[3]{0:T(128)} %hyper.1, f32[2,1680,640]{2,1,0:T(8,128)} %bitcast.6, bf16[2,2048,640]{2,1,0:T(8,128)(2,1)} %x_in.1, ...), custom_call_target="tpu_custom_call" | custom-call | tf_op jit(solution)/shard_map/stats/pallas_call | solution.py:309
  45.4 6.4 %write.1 = (f32[2,1680,640]{2,1,0:T(8,128)}, f32[2,640]{1,0:T(2,128)}, f32[2,1680]{1,0:T(2,128)}, f32[2,1680,640]{2,1,0:T(8,128)}, f32[2,1680]{1,0:T(2,128)}, /*index=5*/f32[2,640]{1,0:T(2,128)}) custom-call(f32[2,1680,640]{2,1,0:T(8,128)S(1)} %get-tuple-element.18.refs_0_, f32[2,640]{1,0:T(2,128)S(1)} %get-tuple-element.19.refs_1_, ...), custom_call_target="tpu_custom_call" | custom-call | tf_op jit(solution)/shard_map/write/pallas_call | solution.py:334

commit v3 on v2

--- a/solution.py
+++ b/solution.py
@@ -20,7 +20,7 @@
 
 def stats_kernel(n_col, n_row, sizes, hyper, w_in, x_in, dy_in, row_in, col_in, w_out, x_out, dy_out, row_out, col_out,
                  wv_in, row_in_new, col_in_new, wv_out, row_out_new, col_out_new,
-                 upd, a_buf, b_buf, row_acc, w_col, inv_n, rx_n, rx_w, rx_s, old_n, old_w,
+                 upd, a_buf, b_buf, row_acc, w_col, inv_n, rx_n, rx_w, rx_a, rx_b, old_n, old_w,
                  a_sem, b_sem, w_sem, send_n, recv_n, send_w, recv_w, send_s, recv_s):
     n_mat, wide, narrow = upd.shape
     layers = n_mat // 2
@@ -47,9 +47,11 @@
     for copy in loads(0):
         copy.start()
     barrier = pltpu.get_barrier_semaphore()
-    for d in range(1, n_dev):
-        peer = lax.rem(me + d, n_dev)
-        pl.semaphore_signal(barrier, inc=1, device_id=(peer // n_row, lax.rem(peer, n_row)), device_id_type=MESH)
+    peers_c = [lax.rem(my_c + d, n_col) for d in range(n_col)]
+    peers_r = [lax.rem(my_r + d, n_row) for d in range(n_row)]
+    peers = [(c, r) for i, c in enumerate(peers_c) for j, r in enumerate(peers_r) if i or j]
+    for peer in peers:
+        pl.semaphore_signal(barrier, inc=1, device_id=peer, device_id_type=MESH)
 
     old_n[...] = jnp.zeros_like(old_n)
     old_w[...] = jnp.zeros_like(old_w)
@@ -69,68 +71,35 @@
     def weights(m):
         return wv_in.at[m % layers] if m < layers else wv_out.at[m % layers]
 
-    def narrow_copy(m, d):
-        peer = lax.rem(my_c + d, n_col)
-        return pltpu.make_async_remote_copy(
-            src_ref=rx_n.at[m, my_c], dst_ref=rx_n.at[m, my_c], send_sem=send_n.at[m, d], recv_sem=recv_n.at[m, my_c],
-            device_id=(peer, my_r), device_id_type=MESH)
-
-    def narrow_arrival(m, d):
-        src = lax.rem(my_c + d, n_col)
-        return pltpu.make_async_remote_copy(
-            src_ref=rx_n.at[m, src], dst_ref=rx_n.at[m, src], send_sem=send_n.at[m, d], recv_sem=recv_n.at[m, src],
-            device_id=(src, my_r), device_id_type=MESH)
-
-    def wide_copy(m, d):
-        peer = lax.rem(my_r + d, n_row)
-        return pltpu.make_async_remote_copy(
-            src_ref=rx_w.at[m, my_r], dst_ref=rx_w.at[m, my_r], send_sem=send_w.at[m, d], recv_sem=recv_w.at[m, my_r],
-            device_id=(my_c, peer), device_id_type=MESH)
-
-    def wide_arrival(m, d):
-        src = lax.rem(my_r + d, n_row)
-        return pltpu.make_async_remote_copy(
-            src_ref=rx_w.at[m, src], dst_ref=rx_w.at[m, src], send_sem=send_w.at[m, d], recv_sem=recv_w.at[m, src],
-            device_id=(my_c, src), device_id_type=MESH)
-
-    def scalar_copy(m, d):
-        peer = lax.rem(me + d, n_dev)
-        return pltpu.make_async_remote_copy(
-            src_ref=rx_s.at[m, me], dst_ref=rx_s.at[m, me], send_sem=send_s.at[m, d], recv_sem=recv_s.at[m, me],
-            device_id=(peer // n_row, lax.rem(peer, n_row)), device_id_type=MESH)
-
-    def scalar_arrival(m, d):
-        src = lax.rem(me + d, n_dev)
-        return pltpu.make_async_remote_copy(
-            src_ref=rx_s.at[m, src], dst_ref=rx_s.at[m, src], send_sem=send_s.at[m, d], recv_sem=recv_s.at[m, src],
-            device_id=(src // n_row, lax.rem(src, n_row)), device_id_type=MESH)
+    def send(buf, index, send_sem, recv_sem, peer):
+        pltpu.make_async_remote_copy(src_ref=buf.at[index], dst_ref=buf.at[index], send_sem=send_sem, recv_sem=recv_sem,
+                                     device_id=peer, device_id_type=MESH).start()
+
+    def wait_bytes(ref, sem):
+        pltpu.make_async_copy(ref, ref, sem).wait()
 
     lane = lax.broadcasted_iota(jnp.int32, (1, LANES), 1)
     zero = jnp.zeros((8, narrow), F32)
     sq_sum = {}
-    norm_sum = {}
     row_mean = {}
 
     group = 16
 
-    def fold(v):
-        return sum(v[r:r + 8] for r in range(8, v.shape[0], 8)) + v[:8]
-
     def scale_group(m, rows, acc):
-        a = jnp.concatenate([w_col[m % 2, rows, :]] * len(nt), axis=1)
-        u = upd[m, rows, :] * a * inv_n[m % 2]
+        u = upd[m, rows, :] * jnp.concatenate([w_col[m, rows, :]] * len(nt), axis=1)
         upd[m, rows, :] = u
-        return acc + fold(u * u)
+        return acc + u * u
 
     def square_group(m, rows, acc):
         v = weights(m)[rows, :]
-        return acc + fold(v * v)
-
-    def all_rows(fn, sums, m):
-        sums[m] = lax.fori_loop(0, wide // group, lambda i, acc: fn(m, pl.ds(pl.multiple_of(i * group, group), group), acc),
-                                zero, unroll=5)
-
-    def products(m, blocks, total):
+        return acc + v * v
+
+    def all_rows(fn, m):
+        return lax.fori_loop(0, wide // group,
+                             lambda i, acc: fn(m, pl.ds(pl.multiple_of(i * group, group), group), acc),
+                             jnp.zeros((group, narrow), F32), unroll=21)
+
+    def products(m, blocks, total, square=None):
         slot = m % 2
         for s, w in blocks:
             g = jnp.dot(b_buf[slot, s:s + w, :], a_buf[slot], preferred_element_type=F32)
@@ -141,6 +110,11 @@
                 part = part + q[:, t:t + tw]
             total = total + jnp.sum(q.reshape(w // 8, 8, narrow), axis=0)
             row_acc[s:s + w, :] = part
+            if square is not None:
+                acc = sq_sum.get(square, jnp.zeros((group, narrow), F32))
+                for r in range(s, s + w, group):
+                    acc = square_group(square, pl.ds(r, group), acc)
+                sq_sum[square] = acc
             for t, tw in tiles:
                 if s < t + tw <= s + w:
                     block = row_acc[t:t + tw, :].T
@@ -152,16 +126,14 @@
         sums = jnp.sum(total, axis=0, keepdims=True)
         for j, (t, tw) in enumerate(nt):
             rx_n[m, my_c, j:j + 1, :] = sums[:, t:t + tw]
-        for d in range(1, n_col):
-            narrow_copy(m, d).start()
-        for d in range(1, n_row):
-            wide_copy(m, d).start()
+        for c in peers_c[1:]:
+            send(rx_n.at[m], my_c, send_n.at[m], recv_n.at[m], (c, my_r))
+        for r in peers_r[1:]:
+            send(rx_w.at[m], my_r, send_w.at[m], recv_w.at[m], (my_c, r))
 
     def wait_moments(m):
-        for d in range(1, n_col):
-            narrow_arrival(m, d).wait_recv()
-        for d in range(1, n_row):
-            wide_arrival(m, d).wait_recv()
+        wait_bytes(rx_n.at[m, pl.ds(0, n_col - 1)], recv_n.at[m])
+        wait_bytes(rx_w.at[m, pl.ds(0, n_row - 1)], recv_w.at[m])
 
     def second_moments(m):
         beta = hyper[0]
@@ -186,28 +158,24 @@
         root = jnp.sqrt(mean)
         scaled = lax.rsqrt(new_n) * root
         for j, (t, tw) in enumerate(nt):
-            inv_n[m % 2, :, t:t + tw] = scaled[j:j + 1, :]
+            inv_n[m, :, t:t + tw] = scaled[j:j + 1, :]
         inv_w = lax.rsqrt(new_w)
         for j, (t, tw) in enumerate(tiles):
-            w_col[m % 2, t:t + tw, :] = jnp.broadcast_to(inv_w[j:j + 1, :tw], (LANES, tw)).T
-
-    def each_peer(fn):
-        def body(d, carry):
-            fn(d)
-            return carry
-        lax.fori_loop(1, n_dev, body, 0)
-
-    def send_scalars(m):
-        norm = jnp.sum(norm_sum[m], keepdims=True)
-        w_sq = jnp.sum(sq_sum[m], keepdims=True)
-        rx_s[m, me] = jnp.where(lane < 32, norm, jnp.where(lane < 64, w_sq, row_mean[m]))
-        each_peer(lambda d: scalar_copy(m, d).start())
-
-    def step_factor(m):
-        each_peer(lambda d: scalar_arrival(m, d).wait_recv())
-        got = rx_s[m]
+            w_col[m, t:t + tw, :] = jnp.broadcast_to(inv_w[j:j + 1, :tw], (LANES, tw)).T
+
+    def send_scalars(group_of, buf, i):
+        for slot, m in enumerate(group_of):
+            norm = jnp.sum(all_rows(scale_group, m), axis=0, keepdims=True) * inv_n[m] * inv_n[m]
+            norm = jnp.sum(norm, axis=1, keepdims=True)
+            w_sq = jnp.sum(jnp.sum(sq_sum[m], axis=0, keepdims=True), axis=1, keepdims=True)
+            buf[me, slot] = jnp.where(lane < 32, norm, jnp.where(lane < 64, w_sq, row_mean[m]))
+        for peer in peers:
+            send(buf, me, send_s.at[i], recv_s.at[i], peer)
+
+    def step_factor(buf, slot):
+        got = buf[:, slot]
         s_full = jnp.sum(jnp.where(lane == 64, jnp.sum(got, axis=0), 0.0), axis=1, keepdims=True) / n_dev
-        own = jnp.sum(jnp.where(lane == 64, rx_s[m, me], 0.0), axis=1, keepdims=True)
+        own = jnp.sum(jnp.where(lane == 64, buf[me, slot], 0.0), axis=1, keepdims=True)
         ratio = s_full[None] / pltpu.roll(got, 64, 2)
         acc = jnp.sum(got * jnp.where(lane[None] < 32, ratio, 1.0), axis=0)
         upd_sq = jnp.sum(jnp.where(lane == 0, acc, 0.0), axis=1, keepdims=True)
@@ -217,15 +185,19 @@
         size = hyper[1] * jnp.maximum(EPS_TWO, w_rms) / jnp.maximum(1.0, upd_rms / hyper[2])
         return size * jnp.sqrt(s_full / own)
 
-    def update(m):
-        k = step_factor(m)
-        w_ref = weights(m)
-
-        def body(i, carry):
-            rows = pl.ds(pl.multiple_of(i * group, group), group)
-            w_ref[rows, :] = w_ref[rows, :] - k * upd[m, rows, :]
-            return carry
-        lax.fori_loop(0, wide // group, body, 0, unroll=5)
+    def update(group_of, buf, i):
+        wait_bytes(buf.at[pl.ds(0, n_dev - 1)], recv_s.at[i])
+        factors = [step_factor(buf, slot) * inv_n[m] for slot, m in enumerate(group_of)]
+        for m, k in zip(group_of, factors):
+            w_ref = weights(m)
+            k = jnp.broadcast_to(k, (8, narrow))
+            k = jnp.concatenate([k] * (group // 8), axis=0)
+
+            def body(step, carry, m=m, w_ref=w_ref, k=k):
+                rows = pl.ds(pl.multiple_of(step * group, group), group)
+                w_ref[rows, :] = w_ref[rows, :] - k * upd[m, rows, :]
+                return carry
+            lax.fori_loop(0, wide // group, body, 0, unroll=21)
 
     last = n_mat - 1
     for m in range(n_mat):
@@ -245,38 +217,47 @@
             for copy in loads(m + 1):
                 copy.start()
         w_copies[m].start()
-        total = products(m, blocks, total)
+        if m:
+            w_copies[m - 1].wait()
+        if m >= 2:
+            wait_moments(m - 2)
+            second_moments(m - 2)
+        total = products(m, blocks, total, m - 1 if m else None)
         if m == 0:
             pl.semaphore_wait(barrier, n_dev - 1)
         send_moments(m, total)
 
+    early, late = list(range(last)), [last]
+    wait_moments(last - 1)
+    second_moments(last - 1)
+    send_scalars(early, rx_a, 0)
+    w_copies[last].wait()
+    sq_sum[last] = all_rows(square_group, last)
+    wait_moments(last)
+    second_moments(last)
+    send_scalars(late, rx_b, 1)
+    update(early, rx_a, 0)
     for m in range(n_mat):
-        w_copies[m].wait()
-        all_rows(square_group, sq_sum, m)
-    for m in range(n_mat):
-        wait_moments(m)
-        second_moments(m)
-        all_rows(scale_group, norm_sum, m)
-        send_scalars(m)
-    for m in range(n_mat):
-        update(m)
-
-    def drain(m, _):
-        for d in range(1, n_col):
-            narrow_copy(m, d).wait_send()
-        for d in range(1, n_row):
-            wide_copy(m, d).wait_send()
-        for d in range(1, n_dev):
-            scalar_copy(m, d).wait_send()
-        return 0
-
-    lax.fori_loop(0, n_mat, drain, 0)
+        wait_bytes(rx_n.at[m, pl.ds(0, n_col - 1)], send_n.at[m])
+        wait_bytes(rx_w.at[m, pl.ds(0, n_row - 1)], send_w.at[m])
+    wait_bytes(rx_a.at[pl.ds(0, n_dev - 1)], send_s.at[0])
+    wait_bytes(rx_b.at[pl.ds(0, n_dev - 1)], send_s.at[1])
+    update(late, rx_b, 1)
 
 
 def write_kernel(*refs):
     count = (len(refs) - 1) // 2
     srcs, dsts, sem = refs[:count], refs[count:2 * count], refs[-1]
-    copies = [pltpu.make_async_copy(src, dst, sem.at[i]) for i, (src, dst) in enumerate(zip(srcs, dsts))]
+    copies = []
+    for src, dst in zip(srcs, dsts):
+        if len(src.shape) == 2:
+            pieces = [(src, dst)]
+        else:
+            rows = src.shape[1] // 2
+            pieces = [(src.at[i, pl.ds(r, rows)], dst.at[i, pl.ds(r, rows)])
+                      for i in range(src.shape[0]) for r in (0, rows)]
+        for src_piece, dst_piece in pieces:
+            copies.append(pltpu.make_async_copy(src_piece, dst_piece, sem.at[len(copies)]))
     for copy in copies:
         copy.start()
     for copy in copies:
@@ -316,17 +297,16 @@
                 pltpu.VMEM((2, tokens, narrow), jnp.bfloat16),
                 pltpu.VMEM((2, wide, tokens), jnp.bfloat16),
                 pltpu.VMEM((wide, LANES), F32),
-                pltpu.VMEM((2, wide, LANES), F32),
-                pltpu.VMEM((2, 1, narrow), F32),
+                pltpu.VMEM((n_mat, wide, LANES), F32),
+                pltpu.VMEM((n_mat, 1, narrow), F32),
                 pltpu.VMEM((n_mat, n_col, nr, LANES), F32),
                 pltpu.VMEM((n_mat, n_row, wr, LANES), F32),
-                pltpu.VMEM((n_mat, n_dev, 1, LANES), F32),
+                pltpu.VMEM((n_dev, n_mat - 1, 1, LANES), F32),
+                pltpu.VMEM((n_dev, 1, 1, LANES), F32),
                 pltpu.VMEM((n_mat, nr, LANES), F32),
                 pltpu.VMEM((n_mat, wr, LANES), F32),
                 dma((2,)), dma((2, len(sizes))), dma((n_mat,)),
-                dma((n_mat, n_col)), dma((n_mat, n_col)),
-                dma((n_mat, n_row)), dma((n_mat, n_row)),
-                dma((n_mat, n_dev)), dma((n_mat, n_dev)),
+                dma((n_mat,)), dma((n_mat,)), dma((n_mat,)), dma((n_mat,)), dma((2,)), dma((2,)),
             ],
             compiler_params=pltpu.CompilerParams(collective_id=0, has_side_effects=True, vmem_limit_bytes=44 << 20),
             name="stats",
@@ -336,7 +316,7 @@
             out_shape=tuple(pltpu.HBM(shape, F32) for shape in shapes),
             in_specs=[vmem] * 6,
             out_specs=(hbm,) * 6,
-            scratch_shapes=[dma((6,))],
+            scratch_shapes=[dma((8 * layers + 4,))],
             compiler_params=pltpu.CompilerParams(vmem_limit_bytes=1 << 20),
             name="write",
         )(*(pltpu.with_memory_space_constraint(v, pltpu.VMEM) for v in results))

time: 52.1 us -> 47.6 us (0.914)
  Pallas kernels: 51.1 us -> 46.6 us
    pallas_call x1, Pallas kernels: 44.7 us -> 40.4 us  [local_step(): pl.pallas_call(functools.partial(stats_kernel, n_col, n_row, sizes), out_...]
where the time goes in v3:
time: 47.6 us; the launch traced here: 47.4 us
  Pallas kernels  46.6 us (98%)
  between operations  0.8 us (2%)
    pallas_call x1, Pallas kernels, local_step(): pl.pallas_call(functools.partial(stats_kernel, n_col, n_row, sizes), out_...  40.4 us
    pallas_call x1, Pallas kernels, local_step(): pl.pallas_call(write_kernel, out_shape=tuple((pltpu.HBM(shape, F32) for s...  6.18 us

profile of v3, /device:TPU:0, one launch (start us, length us, event | category | flops | bytes accessed | tf_op | source)
XLA Modules:
  0.0 47.4 jit_solution(5442018588864882493)
XLA Ops:
  0.6 40.4 %stats.1 = (f32[2,1680,640]{2,1,0:T(8,128)S(1)}, f32[2,640]{1,0:T(2,128)S(1)}, f32[2,1680]{1,0:T(2,128)S(1)}, f32[2,1680,640]{2,1,0:T(8,128)S(1)}, f32[2,1680]{1,0:T(2,128)S(1)}, /*index=5*/f32[2,640]{1,0:T(2,128)S(1)}) custom-call(f32[3]{0:T(128)} %hyper.1, f32[2,1680,640]{2,1,0:T(8,128)} %bitcast.6, bf16[2,2048,640]{2,1,0:T(8,128)(2,1)} %x_in.1, ...), custom_call_target="tpu_custom_call" | custom-call | tf_op jit(solution)/shard_map/stats/pallas_call | solution.py:290
  41.1 6.2 %write.1 = (f32[2,1680,640]{2,1,0:T(8,128)}, f32[2,640]{1,0:T(2,128)}, f32[2,1680]{1,0:T(2,128)}, f32[2,1680,640]{2,1,0:T(8,128)}, f32[2,1680]{1,0:T(2,128)}, /*index=5*/f32[2,640]{1,0:T(2,128)}) custom-call(f32[2,1680,640]{2,1,0:T(8,128)S(1)} %get-tuple-element.18.refs_0_, f32[2,640]{1,0:T(2,128)S(1)} %get-tuple-element.19.refs_1_, ...), custom_call_target="tpu_custom_call" | custom-call | tf_op jit(solution)/shard_map/write/pallas_call | solution.py:314

commit v4 on v3

--- a/solution.py
+++ b/solution.py
@@ -80,24 +80,30 @@
 
     lane = lax.broadcasted_iota(jnp.int32, (1, LANES), 1)
     zero = jnp.zeros((8, narrow), F32)
+    zeros = jnp.zeros((16, narrow), F32)
     sq_sum = {}
     row_mean = {}
 
-    group = 16
-
-    def scale_group(m, rows, acc):
-        u = upd[m, rows, :] * jnp.concatenate([w_col[m, rows, :]] * len(nt), axis=1)
-        upd[m, rows, :] = u
+    group, stretch = 16, 336
+
+    def scale_group(m, at, r, acc):
+        rows = slice(r, r + group)
+        g = at(upd.at[m])
+        u = g[rows, :] * jnp.concatenate([at(w_col.at[m])[rows, :]] * len(nt), axis=1)
+        g[rows, :] = u
         return acc + u * u
 
-    def square_group(m, rows, acc):
-        v = weights(m)[rows, :]
+    def square_group(m, at, r, acc):
+        v = at(weights(m))[r:r + group, :]
         return acc + v * v
 
-    def all_rows(fn, m):
-        return lax.fori_loop(0, wide // group,
-                             lambda i, acc: fn(m, pl.ds(pl.multiple_of(i * group, group), group), acc),
-                             jnp.zeros((group, narrow), F32), unroll=21)
+    def all_rows(fn, init):
+        def body(i, carry):
+            at = lambda ref: ref.at[pl.ds(pl.multiple_of(i * stretch, stretch), stretch)]
+            for r in range(0, stretch, group):
+                carry = fn(at, r, carry)
+            return carry
+        return lax.fori_loop(0, wide // stretch, body, init)
 
     def products(m, blocks, total, square=None):
         slot = m % 2
@@ -111,9 +117,9 @@
             total = total + jnp.sum(q.reshape(w // 8, 8, narrow), axis=0)
             row_acc[s:s + w, :] = part
             if square is not None:
-                acc = sq_sum.get(square, jnp.zeros((group, narrow), F32))
+                acc = sq_sum.get(square, zeros)
                 for r in range(s, s + w, group):
-                    acc = square_group(square, pl.ds(r, group), acc)
+                    acc = square_group(square, lambda ref: ref, r, acc)
                 sq_sum[square] = acc
             for t, tw in tiles:
                 if s < t + tw <= s + w:
@@ -165,7 +171,7 @@
 
     def send_scalars(group_of, buf, i):
         for slot, m in enumerate(group_of):
-            norm = jnp.sum(all_rows(scale_group, m), axis=0, keepdims=True) * inv_n[m] * inv_n[m]
+            norm = jnp.sum(all_rows(functools.partial(scale_group, m), zeros), axis=0, keepdims=True) * inv_n[m] * inv_n[m]
             norm = jnp.sum(norm, axis=1, keepdims=True)
             w_sq = jnp.sum(jnp.sum(sq_sum[m], axis=0, keepdims=True), axis=1, keepdims=True)
             buf[me, slot] = jnp.where(lane < 32, norm, jnp.where(lane < 64, w_sq, row_mean[m]))
@@ -193,11 +199,12 @@
             k = jnp.broadcast_to(k, (8, narrow))
             k = jnp.concatenate([k] * (group // 8), axis=0)
 
-            def body(step, carry, m=m, w_ref=w_ref, k=k):
-                rows = pl.ds(pl.multiple_of(step * group, group), group)
-                w_ref[rows, :] = w_ref[rows, :] - k * upd[m, rows, :]
+            def apply(at, r, carry, m=m, w_ref=w_ref, k=k):
+                rows = slice(r, r + group)
+                w = at(w_ref)
+                w[rows, :] = w[rows, :] - k * at(upd.at[m])[rows, :]
                 return carry
-            lax.fori_loop(0, wide // group, body, 0, unroll=21)
+            all_rows(apply, 0)
 
     last = n_mat - 1
     for m in range(n_mat):
@@ -222,7 +229,7 @@
         if m >= 2:
             wait_moments(m - 2)
             second_moments(m - 2)
-        total = products(m, blocks, total, m - 1 if m else None)
+        total = products(m, blocks, total)
         if m == 0:
             pl.semaphore_wait(barrier, n_dev - 1)
         send_moments(m, total)
@@ -230,9 +237,10 @@
     early, late = list(range(last)), [last]
     wait_moments(last - 1)
     second_moments(last - 1)
+    w_copies[last].wait()
+    for m in range(n_mat):
+        sq_sum[m] = all_rows(functools.partial(square_group, m), zeros)
     send_scalars(early, rx_a, 0)
-    w_copies[last].wait()
-    sq_sum[last] = all_rows(square_group, last)
     wait_moments(last)
     second_moments(last)
     send_scalars(late, rx_b, 1)

time: 47.6 us -> 47.5 us (level)
  no operation moved by 1% of the time
where the time goes in v4:
time: 47.5 us; the launch traced here: 47.3 us
  Pallas kernels  46.5 us (98%)
  between operations  0.8 us (2%)
    pallas_call x1, Pallas kernels, local_step(): pl.pallas_call(functools.partial(stats_kernel, n_col, n_row, sizes), out_...  40.4 us
    pallas_call x1, Pallas kernels, local_step(): pl.pallas_call(write_kernel, out_shape=tuple((pltpu.HBM(shape, F32) for s...  6.18 us

profile of v4, /device:TPU:0, one launch (start us, length us, event | category | flops | bytes accessed | tf_op | source)
XLA Modules:
  0.0 47.3 jit_solution(9241151556212109635)
XLA Ops:
  0.6 40.4 %stats.1 = (f32[2,1680,640]{2,1,0:T(8,128)S(1)}, f32[2,640]{1,0:T(2,128)S(1)}, f32[2,1680]{1,0:T(2,128)S(1)}, f32[2,1680,640]{2,1,0:T(8,128)S(1)}, f32[2,1680]{1,0:T(2,128)S(1)}, /*index=5*/f32[2,640]{1,0:T(2,128)S(1)}) custom-call(f32[3]{0:T(128)} %hyper.1, f32[2,1680,640]{2,1,0:T(8,128)} %bitcast.6, bf16[2,2048,640]{2,1,0:T(8,128)(2,1)} %x_in.1, ...), custom_call_target="tpu_custom_call" | custom-call | tf_op jit(solution)/shard_map/stats/pallas_call | solution.py:298
  41.0 6.2 %write.1 = (f32[2,1680,640]{2,1,0:T(8,128)}, f32[2,640]{1,0:T(2,128)}, f32[2,1680]{1,0:T(2,128)}, f32[2,1680,640]{2,1,0:T(8,128)}, f32[2,1680]{1,0:T(2,128)}, /*index=5*/f32[2,640]{1,0:T(2,128)}) custom-call(f32[2,1680,640]{2,1,0:T(8,128)S(1)} %get-tuple-element.18.refs_0_, f32[2,640]{1,0:T(2,128)S(1)} %get-tuple-element.19.refs_1_, ...), custom_call_target="tpu_custom_call" | custom-call | tf_op jit(solution)/shard_map/write/pallas_call | solution.py:322

commit v5 on v4

--- a/solution.py
+++ b/solution.py
@@ -18,9 +18,9 @@
     return [(start, min(LANES, width - start)) for start in range(0, width, LANES)]
 
 
-def stats_kernel(n_col, n_row, sizes, hyper, w_in, x_in, dy_in, row_in, col_in, w_out, x_out, dy_out, row_out, col_out,
+def stats_kernel(n_col, n_row, sizes, main, hyper, w_in, x_in, dy_in, row_in, col_in, w_out, x_out, dy_out, row_out, col_out,
                  wv_in, row_in_new, col_in_new, wv_out, row_out_new, col_out_new,
-                 upd, a_buf, b_buf, row_acc, w_col, inv_n, rx_n, rx_w, rx_a, rx_b, old_n, old_w,
+                 upd, a_buf, b_buf, a_t, b_t, row_acc, w_col, inv_n, rx_n, rx_w, rx_a, rx_b, old_n, old_w,
                  a_sem, b_sem, w_sem, send_n, recv_n, send_w, recv_w, send_s, recv_s):
     n_mat, wide, narrow = upd.shape
     layers = n_mat // 2
@@ -79,7 +79,6 @@
         pltpu.make_async_copy(ref, ref, sem).wait()
 
     lane = lax.broadcasted_iota(jnp.int32, (1, LANES), 1)
-    zero = jnp.zeros((8, narrow), F32)
     zeros = jnp.zeros((16, narrow), F32)
     sq_sum = {}
     row_mean = {}
@@ -105,17 +104,23 @@
             return carry
         return lax.fori_loop(0, wide // stretch, body, init)
 
-    def products(m, blocks, total, square=None):
+    def products(m, blocks, total, first, square=None):
         slot = m % 2
-        for s, w in blocks:
-            g = jnp.dot(b_buf[slot, s:s + w, :], a_buf[slot], preferred_element_type=F32)
-            upd[m, s:s + w, :] = g
-            q = g * g
-            part = q[:, :LANES]
-            for t, tw in nt[1:]:
-                part = part + q[:, t:t + tw]
-            total = total + jnp.sum(q.reshape(w // 8, 8, narrow), axis=0)
-            row_acc[s:s + w, :] = part
+        if first:
+            a_t[...] = a_buf[slot, :, main:].T
+        for i, (s, w) in enumerate(blocks):
+            block = b_buf.at[slot, pl.ds(s, w)]
+            b_t[i % 2, :, :w] = block[...].T
+            left = jnp.dot(block[...], a_buf[slot, :, :main], preferred_element_type=F32)
+            right = jnp.dot(a_t[...], b_t[i % 2, :, :w], preferred_element_type=F32).T
+            upd[m, s:s + w, :main] = left
+            upd[m, s:s + w, main:] = right
+            q = left * left
+            p = right * right
+            total = total + jnp.concatenate([jnp.sum(v.reshape(w // 8, 8, v.shape[1]), axis=0) for v in (q, p)], axis=1)
+            for t, tw in col_tiles(main):
+                p = p + q[:, t:t + tw]
+            row_acc[s:s + w, :] = p
             if square is not None:
                 acc = sq_sum.get(square, zeros)
                 for r in range(s, s + w, group):
@@ -208,7 +213,7 @@
 
     last = n_mat - 1
     for m in range(n_mat):
-        total = zero
+        total = jnp.zeros((8, narrow), F32)
         copies = loads(m)
         blocks = order
         if m == 0:
@@ -216,8 +221,8 @@
                 copy.wait()
             for copy in loads(1):
                 copy.start()
-            total = products(m, split(0, 208, 224), total)
-            blocks, copies = order[1:-1] + split(order[-1][0], 208, 208), copies[2:]
+            total = products(m, order[:1], total, True)
+            blocks, copies = order[1:], copies[2:]
         for copy in copies:
             copy.wait()
         if 1 <= m < last:
@@ -229,7 +234,7 @@
         if m >= 2:
             wait_moments(m - 2)
             second_moments(m - 2)
-        total = products(m, blocks, total)
+        total = products(m, blocks, total, m > 0)
         if m == 0:
             pl.semaphore_wait(barrier, n_dev - 1)
         send_moments(m, total)
@@ -293,10 +298,11 @@
         dma = pltpu.SemaphoreType.DMA
         nr, wr = 8, 16
         swap = lambda v: jnp.swapaxes(v, 1, 2)
-        sizes = (432, 416, 416, 416)
+        sizes = (512, 512, 512, 144)
+        main = narrow - LANES
         shapes = [v.shape for v in (w_out, row_in, col_in, w_out, row_out, col_out)]
         results = pl.pallas_call(
-            functools.partial(stats_kernel, n_col, n_row, sizes),
+            functools.partial(stats_kernel, n_col, n_row, sizes, main),
             out_shape=tuple(pltpu.VMEM(shape, F32) for shape in shapes),
             in_specs=[smem, hbm, hbm, hbm, vmem, vmem, hbm, hbm, hbm, vmem, vmem],
             out_specs=(vmem,) * 6,
@@ -304,6 +310,8 @@
                 pltpu.VMEM((n_mat, wide, narrow), F32),
                 pltpu.VMEM((2, tokens, narrow), jnp.bfloat16),
                 pltpu.VMEM((2, wide, tokens), jnp.bfloat16),
+                pltpu.VMEM((narrow - main, tokens), jnp.bfloat16),
+                pltpu.VMEM((2, tokens, max(sizes)), jnp.bfloat16),
                 pltpu.VMEM((wide, LANES), F32),
                 pltpu.VMEM((n_mat, wide, LANES), F32),
                 pltpu.VMEM((n_mat, 1, narrow), F32),
@@ -316,7 +324,7 @@
                 dma((2,)), dma((2, len(sizes))), dma((n_mat,)),
                 dma((n_mat,)), dma((n_mat,)), dma((n_mat,)), dma((n_mat,)), dma((2,)), dma((2,)),
             ],
-            compiler_params=pltpu.CompilerParams(collective_id=0, has_side_effects=True, vmem_limit_bytes=44 << 20),
+            compiler_params=pltpu.CompilerParams(collective_id=0, has_side_effects=True, vmem_limit_bytes=46 << 20),
             name="stats",
         )(hyper_params, swap(w_in), x_in, swap(dy_in), row_in, col_in, w_out, swap(x_out), dy_out, row_out, col_out)
         w_in_new, row_in_new, col_in_new, w_out_new, row_out_new, col_out_new = pl.pallas_call(

time: 47.5 us -> 45.9 us (0.966)
  Pallas kernels: 46.5 us -> 45 us
    pallas_call x1, Pallas kernels: 40.4 us -> 38.8 us  [local_step(): pl.pallas_call(functools.partial(stats_kernel, n_col, n_row, sizes, main)...]
where the time goes in v5:
time: 45.9 us; the launch traced here: 45.8 us
  Pallas kernels  45 us (98%)
  between operations  0.8 us (2%)
    pallas_call x1, Pallas kernels, local_step(): pl.pallas_call(functools.partial(stats_kernel, n_col, n_row, sizes, main)...  38.8 us
    pallas_call x1, Pallas kernels, local_step(): pl.pallas_call(write_kernel, out_shape=tuple((pltpu.HBM(shape, F32) for s...  6.18 us

profile of v5, /device:TPU:0, one launch (start us, length us, event | category | flops | bytes accessed | tf_op | source)
XLA Modules:
  0.0 45.8 jit_solution(6330637436453635899)
XLA Ops:
  0.6 38.8 %stats.1 = (f32[2,1680,640]{2,1,0:T(8,128)S(1)}, f32[2,640]{1,0:T(2,128)S(1)}, f32[2,1680]{1,0:T(2,128)S(1)}, f32[2,1680,640]{2,1,0:T(8,128)S(1)}, f32[2,1680]{1,0:T(2,128)S(1)}, /*index=5*/f32[2,640]{1,0:T(2,128)S(1)}) custom-call(f32[3]{0:T(128)} %hyper.1, f32[2,1680,640]{2,1,0:T(8,128)} %bitcast.6, bf16[2,2048,640]{2,1,0:T(8,128)(2,1)} %x_in.1, ...), custom_call_target="tpu_custom_call" | custom-call | tf_op jit(solution)/shard_map/stats/pallas_call | solution.py:304
  39.4 6.2 %write.1 = (f32[2,1680,640]{2,1,0:T(8,128)}, f32[2,640]{1,0:T(2,128)}, f32[2,1680]{1,0:T(2,128)}, f32[2,1680,640]{2,1,0:T(8,128)}, f32[2,1680]{1,0:T(2,128)}, /*index=5*/f32[2,640]{1,0:T(2,128)}) custom-call(f32[2,1680,640]{2,1,0:T(8,128)S(1)} %get-tuple-element.18.refs_0_, f32[2,640]{1,0:T(2,128)S(1)} %get-tuple-element.19.refs_1_, ...), custom_call_target="tpu_custom_call" | custom-call | tf_op jit(solution)/shard_map/write/pallas_call | solution.py:330

commit v6 on v5

--- a/solution.py
+++ b/solution.py
@@ -19,11 +19,12 @@
 
 
 def stats_kernel(n_col, n_row, sizes, main, hyper, w_in, x_in, dy_in, row_in, col_in, w_out, x_out, dy_out, row_out, col_out,
-                 wv_in, row_in_new, col_in_new, wv_out, row_out_new, col_out_new,
+                 wv_in, row_in_new, col_in_new, wv_out, row_out_new, col_out_new, last_grad, last_factor,
                  upd, a_buf, b_buf, a_t, b_t, row_acc, w_col, inv_n, rx_n, rx_w, rx_a, rx_b, old_n, old_w,
                  a_sem, b_sem, w_sem, send_n, recv_n, send_w, recv_w, send_s, recv_s):
-    n_mat, wide, narrow = upd.shape
-    layers = n_mat // 2
+    layers, wide, narrow = wv_in.shape
+    n_mat = 2 * layers
+    last = n_mat - 1
     full_narrow, full_wide = narrow * n_row, wide * n_col
     n_total = float(full_narrow * full_wide)
     my_c, my_r = lax.axis_index("col"), lax.axis_index("row")
@@ -47,9 +48,12 @@
     for copy in loads(0):
         copy.start()
     barrier = pltpu.get_barrier_semaphore()
-    peers_c = [lax.rem(my_c + d, n_col) for d in range(n_col)]
-    peers_r = [lax.rem(my_r + d, n_row) for d in range(n_row)]
-    peers = [(c, r) for i, c in enumerate(peers_c) for j, r in enumerate(peers_r) if i or j]
+    flip = lambda v: v + 1 - 2 * lax.rem(v, 2)
+    peers_c = [(n_col - 1 - my_c, 2), (lax.rem(my_c + 2, n_col), 1), (flip(my_c), 1), (my_c, 0)]
+    peers_r = [(n_row - 1 - my_r, 1), (lax.rem(my_r + 2, n_row), 1), (flip(my_r), 0), (my_r, 0)]
+    peers = sorted(((hops_c + hops_r, i, j) for i, (_, hops_c) in enumerate(peers_c) for j, (_, hops_r) in enumerate(peers_r)
+                    if (i, j) != (3, 3)), reverse=True)
+    peers = [(peers_c[i][0], peers_r[j][0]) for _, i, j in peers]
     for peer in peers:
         pl.semaphore_signal(barrier, inc=1, device_id=peer, device_id_type=MESH)
 
@@ -68,6 +72,9 @@
     w_copies = ([pltpu.make_async_copy(w_in.at[i], wv_in.at[i], w_sem.at[i]) for i in range(layers)]
                 + [pltpu.make_async_copy(w_out.at[i], wv_out.at[i], w_sem.at[layers + i]) for i in range(layers)])
 
+    def grad(m):
+        return upd.at[m] if m < last else last_grad
+
     def weights(m):
         return wv_in.at[m % layers] if m < layers else wv_out.at[m % layers]
 
@@ -78,7 +85,6 @@
     def wait_bytes(ref, sem):
         pltpu.make_async_copy(ref, ref, sem).wait()
 
-    lane = lax.broadcasted_iota(jnp.int32, (1, LANES), 1)
     zeros = jnp.zeros((16, narrow), F32)
     sq_sum = {}
     row_mean = {}
@@ -87,7 +93,7 @@
 
     def scale_group(m, at, r, acc):
         rows = slice(r, r + group)
-        g = at(upd.at[m])
+        g = at(grad(m))
         u = g[rows, :] * jnp.concatenate([at(w_col.at[m])[rows, :]] * len(nt), axis=1)
         g[rows, :] = u
         return acc + u * u
@@ -104,7 +110,7 @@
             return carry
         return lax.fori_loop(0, wide // stretch, body, init)
 
-    def products(m, blocks, total, first, square=None):
+    def products(m, blocks, total, first):
         slot = m % 2
         if first:
             a_t[...] = a_buf[slot, :, main:].T
@@ -113,19 +119,14 @@
             b_t[i % 2, :, :w] = block[...].T
             left = jnp.dot(block[...], a_buf[slot, :, :main], preferred_element_type=F32)
             right = jnp.dot(a_t[...], b_t[i % 2, :, :w], preferred_element_type=F32).T
-            upd[m, s:s + w, :main] = left
-            upd[m, s:s + w, main:] = right
+            grad(m)[s:s + w, :main] = left
+            grad(m)[s:s + w, main:] = right
             q = left * left
             p = right * right
             total = total + jnp.concatenate([jnp.sum(v.reshape(w // 8, 8, v.shape[1]), axis=0) for v in (q, p)], axis=1)
             for t, tw in col_tiles(main):
                 p = p + q[:, t:t + tw]
             row_acc[s:s + w, :] = p
-            if square is not None:
-                acc = sq_sum.get(square, zeros)
-                for r in range(s, s + w, group):
-                    acc = square_group(square, lambda ref: ref, r, acc)
-                sq_sum[square] = acc
             for t, tw in tiles:
                 if s < t + tw <= s + w:
                     block = row_acc[t:t + tw, :].T
@@ -137,9 +138,9 @@
         sums = jnp.sum(total, axis=0, keepdims=True)
         for j, (t, tw) in enumerate(nt):
             rx_n[m, my_c, j:j + 1, :] = sums[:, t:t + tw]
-        for c in peers_c[1:]:
+        for c, _ in peers_c[:-1]:
             send(rx_n.at[m], my_c, send_n.at[m], recv_n.at[m], (c, my_r))
-        for r in peers_r[1:]:
+        for r, _ in peers_r[:-1]:
             send(rx_w.at[m], my_r, send_w.at[m], recv_w.at[m], (my_c, r))
 
     def wait_moments(m):
@@ -179,18 +180,17 @@
             norm = jnp.sum(all_rows(functools.partial(scale_group, m), zeros), axis=0, keepdims=True) * inv_n[m] * inv_n[m]
             norm = jnp.sum(norm, axis=1, keepdims=True)
             w_sq = jnp.sum(jnp.sum(sq_sum[m], axis=0, keepdims=True), axis=1, keepdims=True)
-            buf[me, slot] = jnp.where(lane < 32, norm, jnp.where(lane < 64, w_sq, row_mean[m]))
+            for row, v in enumerate((norm, w_sq, row_mean[m])):
+                buf[me, 3 * slot + row] = jnp.broadcast_to(v, (1, LANES))
         for peer in peers:
             send(buf, me, send_s.at[i], recv_s.at[i], peer)
 
     def step_factor(buf, slot):
-        got = buf[:, slot]
-        s_full = jnp.sum(jnp.where(lane == 64, jnp.sum(got, axis=0), 0.0), axis=1, keepdims=True) / n_dev
-        own = jnp.sum(jnp.where(lane == 64, buf[me, slot], 0.0), axis=1, keepdims=True)
-        ratio = s_full[None] / pltpu.roll(got, 64, 2)
-        acc = jnp.sum(got * jnp.where(lane[None] < 32, ratio, 1.0), axis=0)
-        upd_sq = jnp.sum(jnp.where(lane == 0, acc, 0.0), axis=1, keepdims=True)
-        w_sq = jnp.sum(jnp.where(lane == 32, acc, 0.0), axis=1, keepdims=True)
+        norms, w_sqs, means = (buf[:, 3 * slot + row] for row in range(3))
+        s_full = jnp.sum(means, axis=0) / n_dev
+        own = buf[me, 3 * slot + 2]
+        upd_sq = jnp.sum(norms * (s_full[None] / means), axis=0)
+        w_sq = jnp.sum(w_sqs, axis=0)
         upd_rms = jnp.sqrt(upd_sq / n_total)
         w_rms = jnp.sqrt(w_sq / n_total)
         size = hyper[1] * jnp.maximum(EPS_TWO, w_rms) / jnp.maximum(1.0, upd_rms / hyper[2])
@@ -198,8 +198,11 @@
 
     def update(group_of, buf, i):
         wait_bytes(buf.at[pl.ds(0, n_dev - 1)], recv_s.at[i])
-        factors = [step_factor(buf, slot) * inv_n[m] for slot, m in enumerate(group_of)]
+        factors = [jnp.concatenate([step_factor(buf, slot)] * len(nt), axis=1) * inv_n[m] for slot, m in enumerate(group_of)]
         for m, k in zip(group_of, factors):
+            if m == last:
+                last_factor[...] = k
+                return
             w_ref = weights(m)
             k = jnp.broadcast_to(k, (8, narrow))
             k = jnp.concatenate([k] * (group // 8), axis=0)
@@ -207,11 +210,10 @@
             def apply(at, r, carry, m=m, w_ref=w_ref, k=k):
                 rows = slice(r, r + group)
                 w = at(w_ref)
-                w[rows, :] = w[rows, :] - k * at(upd.at[m])[rows, :]
+                w[rows, :] = w[rows, :] - k * at(grad(m))[rows, :]
                 return carry
             all_rows(apply, 0)
 
-    last = n_mat - 1
     for m in range(n_mat):
         total = jnp.zeros((8, narrow), F32)
         copies = loads(m)
@@ -229,8 +231,6 @@
             for copy in loads(m + 1):
                 copy.start()
         w_copies[m].start()
-        if m:
-            w_copies[m - 1].wait()
         if m >= 2:
             wait_moments(m - 2)
             second_moments(m - 2)
@@ -242,8 +242,8 @@
     early, late = list(range(last)), [last]
     wait_moments(last - 1)
     second_moments(last - 1)
-    w_copies[last].wait()
     for m in range(n_mat):
+        w_copies[m].wait()
         sq_sum[m] = all_rows(functools.partial(square_group, m), zeros)
     send_scalars(early, rx_a, 0)
     wait_moments(last)
@@ -259,22 +259,31 @@
 
 
 def write_kernel(*refs):
-    count = (len(refs) - 1) // 2
-    srcs, dsts, sem = refs[:count], refs[count:2 * count], refs[-1]
+    count = (len(refs) - 4) // 2
+    srcs, (grad, factor), dsts, (stage, sem) = refs[:count], refs[count:count + 2], refs[count + 2:-2], refs[-2:]
+    layers, wide, _ = srcs[3].shape
     copies = []
-    for src, dst in zip(srcs, dsts):
-        if len(src.shape) == 2:
-            pieces = [(src, dst)]
-        else:
-            rows = src.shape[1] // 2
-            pieces = [(src.at[i, pl.ds(r, rows)], dst.at[i, pl.ds(r, rows)])
-                      for i in range(src.shape[0]) for r in (0, rows)]
-        for src_piece, dst_piece in pieces:
-            copies.append(pltpu.make_async_copy(src_piece, dst_piece, sem.at[len(copies)]))
-    for copy in copies:
-        copy.start()
-    for copy in copies:
-        copy.wait()
+
+    def copy(src, dst):
+        copies.append(pltpu.make_async_copy(src, dst, sem.at[len(copies)]))
+        copies[-1].start()
+
+    rows = wide // 2
+    for src, dst in ((srcs[0], dsts[0]), (srcs[3], dsts[3])):
+        for i in range(layers):
+            if src is not srcs[3] or i < layers - 1:
+                for r in (0, rows):
+                    copy(src.at[i, pl.ds(r, rows)], dst.at[i, pl.ds(r, rows)])
+    for i in (1, 2, 4, 5):
+        copy(srcs[i], dsts[i])
+    step = wide // 5
+    k = factor[...]
+    for r in range(0, wide, step):
+        for t in range(r, r + step, 16):
+            stage[t:t + 16, :] = srcs[3][layers - 1, t:t + 16, :] - k * grad[t:t + 16, :]
+        copy(stage.at[pl.ds(r, step)], dsts[3].at[layers - 1, pl.ds(r, step)])
+    for item in copies:
+        item.wait()
 
 
 def solution(mesh):
@@ -303,11 +312,11 @@
         shapes = [v.shape for v in (w_out, row_in, col_in, w_out, row_out, col_out)]
         results = pl.pallas_call(
             functools.partial(stats_kernel, n_col, n_row, sizes, main),
-            out_shape=tuple(pltpu.VMEM(shape, F32) for shape in shapes),
+            out_shape=tuple(pltpu.VMEM(shape, F32) for shape in shapes + [w_out.shape[1:], (1, narrow)]),
             in_specs=[smem, hbm, hbm, hbm, vmem, vmem, hbm, hbm, hbm, vmem, vmem],
-            out_specs=(vmem,) * 6,
+            out_specs=(vmem,) * 8,
             scratch_shapes=[
-                pltpu.VMEM((n_mat, wide, narrow), F32),
+                pltpu.VMEM((n_mat - 1, wide, narrow), F32),
                 pltpu.VMEM((2, tokens, narrow), jnp.bfloat16),
                 pltpu.VMEM((2, wide, tokens), jnp.bfloat16),
                 pltpu.VMEM((narrow - main, tokens), jnp.bfloat16),
@@ -317,23 +326,23 @@
                 pltpu.VMEM((n_mat, 1, narrow), F32),
                 pltpu.VMEM((n_mat, n_col, nr, LANES), F32),
                 pltpu.VMEM((n_mat, n_row, wr, LANES), F32),
-                pltpu.VMEM((n_dev, n_mat - 1, 1, LANES), F32),
-                pltpu.VMEM((n_dev, 1, 1, LANES), F32),
+                pltpu.VMEM((n_dev, 3 * (n_mat - 1), 1, LANES), F32),
+                pltpu.VMEM((n_dev, 3, 1, LANES), F32),
                 pltpu.VMEM((n_mat, nr, LANES), F32),
                 pltpu.VMEM((n_mat, wr, LANES), F32),
                 dma((2,)), dma((2, len(sizes))), dma((n_mat,)),
                 dma((n_mat,)), dma((n_mat,)), dma((n_mat,)), dma((n_mat,)), dma((2,)), dma((2,)),
             ],
-            compiler_params=pltpu.CompilerParams(collective_id=0, has_side_effects=True, vmem_limit_bytes=46 << 20),
+            compiler_params=pltpu.CompilerParams(collective_id=0, has_side_effects=True, vmem_limit_bytes=42 << 20),
             name="stats",
         )(hyper_params, swap(w_in), x_in, swap(dy_in), row_in, col_in, w_out, swap(x_out), dy_out, row_out, col_out)
         w_in_new, row_in_new, col_in_new, w_out_new, row_out_new, col_out_new = pl.pallas_call(
             write_kernel,
             out_shape=tuple(pltpu.HBM(shape, F32) for shape in shapes),
-            in_specs=[vmem] * 6,
+            in_specs=[vmem] * 8,
             out_specs=(hbm,) * 6,
-            scratch_shapes=[dma((8 * layers + 4,))],
-            compiler_params=pltpu.CompilerParams(vmem_limit_bytes=1 << 20),
+            scratch_shapes=[pltpu.VMEM(w_out.shape[1:], F32), dma((4 * layers + 7,))],
+            compiler_params=pltpu.CompilerParams(vmem_limit_bytes=6 << 20),
             name="write",
         )(*(pltpu.with_memory_space_constraint(v, pltpu.VMEM) for v in results))
         return swap(w_in_new), row_in_new, col_in_new, w_out_new, row_out_new, col_out_new

time: 45.9 us -> 44.9 us (0.978)
  Pallas kernels: 45 us -> 43.9 us
    pallas_call x1, Pallas kernels: 38.8 us -> 37.8 us  [local_step(): pl.pallas_call(functools.partial(stats_kernel, n_col, n_row, sizes, main)...]
where the time goes in v6:
time: 44.9 us; the launch traced here: 44.7 us
  Pallas kernels  43.9 us (98%)
  between operations  0.8 us (2%)
    pallas_call x1, Pallas kernels, local_step(): pl.pallas_call(functools.partial(stats_kernel, n_col, n_row, sizes, main)...  37.8 us
    pallas_call x1, Pallas kernels, local_step(): pl.pallas_call(write_kernel, out_shape=tuple((pltpu.HBM(shape, F32) for s...  6.09 us

profile of v6, /device:TPU:0, one launch (start us, length us, event | category | flops | bytes accessed | tf_op | source)
XLA Modules:
  0.0 44.7 jit_solution(5282793829421399827)
XLA Ops:
  0.6 37.8 %stats.1 = (f32[2,1680,640]{2,1,0:T(8,128)S(1)}, f32[2,640]{1,0:T(2,128)S(1)}, f32[2,1680]{1,0:T(2,128)S(1)}, f32[2,1680,640]{2,1,0:T(8,128)S(1)}, f32[2,1680]{1...) custom-call(f32[3]{0:T(128)} %hyper.1, f32[2,1680,640]{2,1,0:T(8,128)} %bitcast.6, ...), custom_call_target="tpu_custom_call" | custom-call | tf_op jit(solution)/shard_map/stats/pallas_call | solution.py:313
  38.4 6.1 %write.1 = (f32[2,1680,640]{2,1,0:T(8,128)}, f32[2,640]{1,0:T(2,128)}, f32[2,1680]{1,0:T(2,128)}, f32[2,1680,640]{2,1,0:T(8,128)}, f32[2,1680]{1,0:T(2,128)}, /*index=5*/f32[2,640]{1,0:T(2,128)}) custom-call(f32[2,1680,640]{2,1,0:T(8,128)S(1)} %get-tuple-element.20.refs_0_, f32[2,640]{1,0:T(2,128)S(1)} %get-tuple-element.21.refs_1_, ...), custom_call_target="tpu_custom_call" | custom-call | tf_op jit(solution)/shard_map/write/pallas_call | solution.py:339

commit v7 on v6

--- a/solution.py
+++ b/solution.py
@@ -25,6 +25,7 @@
     layers, wide, narrow = wv_in.shape
     n_mat = 2 * layers
     last = n_mat - 1
+    kept = n_mat - layers
     full_narrow, full_wide = narrow * n_row, wide * n_col
     n_total = float(full_narrow * full_wide)
     my_c, my_r = lax.axis_index("col"), lax.axis_index("row")
@@ -73,7 +74,7 @@
                 + [pltpu.make_async_copy(w_out.at[i], wv_out.at[i], w_sem.at[layers + i]) for i in range(layers)])
 
     def grad(m):
-        return upd.at[m] if m < last else last_grad
+        return upd.at[m] if m < kept else last_grad.at[m - kept]
 
     def weights(m):
         return wv_in.at[m % layers] if m < layers else wv_out.at[m % layers]
@@ -101,6 +102,9 @@
     def square_group(m, at, r, acc):
         v = at(weights(m))[r:r + group, :]
         return acc + v * v
+
+    def both_group(m, at, r, accs):
+        return scale_group(m, at, r, accs[0]), square_group(m, at, r, accs[1])
 
     def all_rows(fn, init):
         def body(i, carry):
@@ -177,7 +181,11 @@
 
     def send_scalars(group_of, buf, i):
         for slot, m in enumerate(group_of):
-            norm = jnp.sum(all_rows(functools.partial(scale_group, m), zeros), axis=0, keepdims=True) * inv_n[m] * inv_n[m]
+            if m in sq_sum:
+                norm = all_rows(functools.partial(scale_group, m), zeros)
+            else:
+                norm, sq_sum[m] = all_rows(functools.partial(both_group, m), (zeros, zeros))
+            norm = jnp.sum(norm, axis=0, keepdims=True) * inv_n[m] * inv_n[m]
             norm = jnp.sum(norm, axis=1, keepdims=True)
             w_sq = jnp.sum(jnp.sum(sq_sum[m], axis=0, keepdims=True), axis=1, keepdims=True)
             for row, v in enumerate((norm, w_sq, row_mean[m])):
@@ -200,9 +208,9 @@
         wait_bytes(buf.at[pl.ds(0, n_dev - 1)], recv_s.at[i])
         factors = [jnp.concatenate([step_factor(buf, slot)] * len(nt), axis=1) * inv_n[m] for slot, m in enumerate(group_of)]
         for m, k in zip(group_of, factors):
-            if m == last:
-                last_factor[...] = k
-                return
+            if m >= kept:
+                last_factor[m - kept] = k
+                continue
             w_ref = weights(m)
             k = jnp.broadcast_to(k, (8, narrow))
             k = jnp.concatenate([k] * (group // 8), axis=0)
@@ -240,12 +248,12 @@
         send_moments(m, total)
 
     early, late = list(range(last)), [last]
+    for copy in w_copies:
+        copy.wait()
     wait_moments(last - 1)
     second_moments(last - 1)
-    for m in range(n_mat):
-        w_copies[m].wait()
-        sq_sum[m] = all_rows(functools.partial(square_group, m), zeros)
     send_scalars(early, rx_a, 0)
+    sq_sum[last] = all_rows(functools.partial(square_group, last), zeros)
     wait_moments(last)
     second_moments(last)
     send_scalars(late, rx_b, 1)
@@ -269,19 +277,18 @@
         copies[-1].start()
 
     rows = wide // 2
-    for src, dst in ((srcs[0], dsts[0]), (srcs[3], dsts[3])):
-        for i in range(layers):
-            if src is not srcs[3] or i < layers - 1:
-                for r in (0, rows):
-                    copy(src.at[i, pl.ds(r, rows)], dst.at[i, pl.ds(r, rows)])
+    for i in range(layers):
+        for r in (0, rows):
+            copy(srcs[0].at[i, pl.ds(r, rows)], dsts[0].at[i, pl.ds(r, rows)])
     for i in (1, 2, 4, 5):
         copy(srcs[i], dsts[i])
     step = wide // 5
-    k = factor[...]
-    for r in range(0, wide, step):
-        for t in range(r, r + step, 16):
-            stage[t:t + 16, :] = srcs[3][layers - 1, t:t + 16, :] - k * grad[t:t + 16, :]
-        copy(stage.at[pl.ds(r, step)], dsts[3].at[layers - 1, pl.ds(r, step)])
+    for i in range(layers):
+        k = factor[i]
+        for r in range(0, wide, step):
+            for t in range(r, r + step, 16):
+                stage[i, t:t + 16, :] = srcs[3][i, t:t + 16, :] - k * grad[i, t:t + 16, :]
+            copy(stage.at[i, pl.ds(r, step)], dsts[3].at[i, pl.ds(r, step)])
     for item in copies:
         item.wait()
 
@@ -312,11 +319,11 @@
         shapes = [v.shape for v in (w_out, row_in, col_in, w_out, row_out, col_out)]
         results = pl.pallas_call(
             functools.partial(stats_kernel, n_col, n_row, sizes, main),
-            out_shape=tuple(pltpu.VMEM(shape, F32) for shape in shapes + [w_out.shape[1:], (1, narrow)]),
+            out_shape=tuple(pltpu.VMEM(shape, F32) for shape in shapes + [w_out.shape, (layers, 1, narrow)]),
             in_specs=[smem, hbm, hbm, hbm, vmem, vmem, hbm, hbm, hbm, vmem, vmem],
             out_specs=(vmem,) * 8,
             scratch_shapes=[
-                pltpu.VMEM((n_mat - 1, wide, narrow), F32),
+                pltpu.VMEM((n_mat - layers, wide, narrow), F32),
                 pltpu.VMEM((2, tokens, narrow), jnp.bfloat16),
                 pltpu.VMEM((2, wide, tokens), jnp.bfloat16),
                 pltpu.VMEM((narrow - main, tokens), jnp.bfloat16),
@@ -333,7 +340,7 @@
                 dma((2,)), dma((2, len(sizes))), dma((n_mat,)),
                 dma((n_mat,)), dma((n_mat,)), dma((n_mat,)), dma((n_mat,)), dma((2,)), dma((2,)),
             ],
-            compiler_params=pltpu.CompilerParams(collective_id=0, has_side_effects=True, vmem_limit_bytes=42 << 20),
+            compiler_params=pltpu.CompilerParams(collective_id=0, has_side_effects=True, vmem_limit_bytes=38 << 20),
             name="stats",
         )(hyper_params, swap(w_in), x_in, swap(dy_in), row_in, col_in, w_out, swap(x_out), dy_out, row_out, col_out)
         w_in_new, row_in_new, col_in_new, w_out_new, row_out_new, col_out_new = pl.pallas_call(
@@ -341,8 +348,8 @@
             out_shape=tuple(pltpu.HBM(shape, F32) for shape in shapes),
             in_specs=[vmem] * 8,
             out_specs=(hbm,) * 6,
-            scratch_shapes=[pltpu.VMEM(w_out.shape[1:], F32), dma((4 * layers + 7,))],
-            compiler_params=pltpu.CompilerParams(vmem_limit_bytes=6 << 20),
+            scratch_shapes=[pltpu.VMEM(w_out.shape, F32), dma((7 * layers + 4,))],
+            compiler_params=pltpu.CompilerParams(vmem_limit_bytes=10 << 20),
             name="write",
         )(*(pltpu.with_memory_space_constraint(v, pltpu.VMEM) for v in results))
         return swap(w_in_new), row_in_new, col_in_new, w_out_new, row_out_new, col_out_new

time: 44.9 us -> 44 us (0.980)
  Pallas kernels: 43.9 us -> 43 us
    pallas_call x1, Pallas kernels: 37.8 us -> 36.9 us  [local_step(): pl.pallas_call(functools.partial(stats_kernel, n_col, n_row, sizes, main)...]
where the time goes in v7:
time: 44 us; the launch traced here: 43.8 us
  Pallas kernels  43 us (98%)
  between operations  0.8 us (2%)
    pallas_call x1, Pallas kernels, local_step(): pl.pallas_call(functools.partial(stats_kernel, n_col, n_row, sizes, main)...  36.9 us
    pallas_call x1, Pallas kernels, local_step(): pl.pallas_call(write_kernel, out_shape=tuple((pltpu.HBM(shape, F32) for s...  6.12 us

profile of v7, /device:TPU:0, one launch (start us, length us, event | category | flops | bytes accessed | tf_op | source)
XLA Modules:
  0.0 43.8 jit_solution(2198907806713256288)
XLA Ops:
  0.6 36.9 %stats.1 = (f32[2,1680,640]{2,1,0:T(8,128)S(1)}, f32[2,640]{1,0:T(2,128)S(1)}, f32[2,1680]{1,0:T(2,128)S(1)}, f32[2,1680,640]{2,1,0:T(8,128)S(1)}, f32[2,1680]{1...) custom-call(f32[3]{0:T(128)} %hyper.1, f32[2,1680,640]{2,1,0:T(8,128)} %bitcast.6, ...), custom_call_target="tpu_custom_call" | custom-call | tf_op jit(solution)/shard_map/stats/pallas_call | solution.py:320
  37.5 6.1 %write.1 = (f32[2,1680,640]{2,1,0:T(8,128)}, f32[2,640]{1,0:T(2,128)}, f32[2,1680]{1,0:T(2,128)}, f32[2,1680,640]{2,1,0:T(8,128)}, f32[2,1680]{1,0:T(2,128)}, /*index=5*/f32[2,640]{1,0:T(2,128)}) custom-call(f32[2,1680,640]{2,1,0:T(8,128)S(1)} %get-tuple-element.20.refs_0_, f32[2,640]{1,0:T(2,128)S(1)} %get-tuple-element.21.refs_1_, ...), custom_call_target="tpu_custom_call" | custom-call | tf_op jit(solution)/shard_map/write/pallas_call | solution.py:346

commit v8 on v7

--- a/solution.py
+++ b/solution.py
@@ -25,7 +25,7 @@
     layers, wide, narrow = wv_in.shape
     n_mat = 2 * layers
     last = n_mat - 1
-    kept = n_mat - layers
+    kept = 1
     full_narrow, full_wide = narrow * n_row, wide * n_col
     n_total = float(full_narrow * full_wide)
     my_c, my_r = lax.axis_index("col"), lax.axis_index("row")
@@ -267,8 +267,7 @@
 
 
 def write_kernel(*refs):
-    count = (len(refs) - 4) // 2
-    srcs, (grad, factor), dsts, (stage, sem) = refs[:count], refs[count:count + 2], refs[count + 2:-2], refs[-2:]
+    srcs, (_, factor), dsts, (grad, sem) = refs[:6], refs[6:8], refs[8:14], refs[14:]
     layers, wide, _ = srcs[3].shape
     copies = []
 
@@ -277,18 +276,18 @@
         copies[-1].start()
 
     rows = wide // 2
-    for i in range(layers):
-        for r in (0, rows):
-            copy(srcs[0].at[i, pl.ds(r, rows)], dsts[0].at[i, pl.ds(r, rows)])
+    for r in (0, rows):
+        copy(srcs[0].at[0, pl.ds(r, rows)], dsts[0].at[0, pl.ds(r, rows)])
     for i in (1, 2, 4, 5):
         copy(srcs[i], dsts[i])
     step = wide // 5
-    for i in range(layers):
-        k = factor[i]
+    for m in range(1, 2 * layers):
+        k = factor[m - 1]
+        src, dst = (srcs[0].at[m], dsts[0].at[m]) if m < layers else (srcs[3].at[m - layers], dsts[3].at[m - layers])
         for r in range(0, wide, step):
             for t in range(r, r + step, 16):
-                stage[i, t:t + 16, :] = srcs[3][i, t:t + 16, :] - k * grad[i, t:t + 16, :]
-            copy(stage.at[i, pl.ds(r, step)], dsts[3].at[i, pl.ds(r, step)])
+                grad[m - 1, t:t + 16, :] = src[t:t + 16, :] - k * grad[m - 1, t:t + 16, :]
+            copy(grad.at[m - 1, pl.ds(r, step)], dst.at[pl.ds(r, step)])
     for item in copies:
         item.wait()
 
@@ -319,11 +318,11 @@
         shapes = [v.shape for v in (w_out, row_in, col_in, w_out, row_out, col_out)]
         results = pl.pallas_call(
             functools.partial(stats_kernel, n_col, n_row, sizes, main),
-            out_shape=tuple(pltpu.VMEM(shape, F32) for shape in shapes + [w_out.shape, (layers, 1, narrow)]),
+            out_shape=tuple(pltpu.VMEM(shape, F32) for shape in shapes + [(n_mat - 1, wide, narrow), (n_mat - 1, 1, narrow)]),
             in_specs=[smem, hbm, hbm, hbm, vmem, vmem, hbm, hbm, hbm, vmem, vmem],
             out_specs=(vmem,) * 8,
             scratch_shapes=[
-                pltpu.VMEM((n_mat - layers, wide, narrow), F32),
+                pltpu.VMEM((1, wide, narrow), F32),
                 pltpu.VMEM((2, tokens, narrow), jnp.bfloat16),
                 pltpu.VMEM((2, wide, tokens), jnp.bfloat16),
                 pltpu.VMEM((narrow - main, tokens), jnp.bfloat16),
@@ -340,16 +339,17 @@
                 dma((2,)), dma((2, len(sizes))), dma((n_mat,)),
                 dma((n_mat,)), dma((n_mat,)), dma((n_mat,)), dma((n_mat,)), dma((2,)), dma((2,)),
             ],
-            compiler_params=pltpu.CompilerParams(collective_id=0, has_side_effects=True, vmem_limit_bytes=38 << 20),
+            compiler_params=pltpu.CompilerParams(collective_id=0, has_side_effects=True, vmem_limit_bytes=34 << 20),
             name="stats",
         )(hyper_params, swap(w_in), x_in, swap(dy_in), row_in, col_in, w_out, swap(x_out), dy_out, row_out, col_out)
-        w_in_new, row_in_new, col_in_new, w_out_new, row_out_new, col_out_new = pl.pallas_call(
+        w_in_new, row_in_new, col_in_new, w_out_new, row_out_new, col_out_new, _ = pl.pallas_call(
             write_kernel,
-            out_shape=tuple(pltpu.HBM(shape, F32) for shape in shapes),
+            out_shape=tuple(pltpu.HBM(shape, F32) for shape in shapes) + (pltpu.VMEM((n_mat - 1, wide, narrow), F32),),
             in_specs=[vmem] * 8,
-            out_specs=(hbm,) * 6,
-            scratch_shapes=[pltpu.VMEM(w_out.shape, F32), dma((7 * layers + 4,))],
-            compiler_params=pltpu.CompilerParams(vmem_limit_bytes=10 << 20),
+            out_specs=(hbm,) * 6 + (vmem,),
+            scratch_shapes=[dma((5 * n_mat + 1,))],
+            input_output_aliases={6: 6},
+            compiler_params=pltpu.CompilerParams(vmem_limit_bytes=1 << 20),
             name="write",
         )(*(pltpu.with_memory_space_constraint(v, pltpu.VMEM) for v in results))
         return swap(w_in_new), row_in_new, col_in_new, w_out_new, row_out_new, col_out_new

time: 44 us -> 44.1 us (level)
  no operation moved by 1% of the time
where the time goes in v8:
time: 44.1 us; the launch traced here: 43.9 us
  Pallas kernels  43.1 us (98%)
  between operations  0.8 us (2%)
    pallas_call x1, Pallas kernels, local_step(): pl.pallas_call(functools.partial(stats_kernel, n_col, n_row, sizes, main)...  37 us
    pallas_call x1, Pallas kernels, local_step(): pl.pallas_call(write_kernel, out_shape=tuple((pltpu.HBM(shape, F32) for s...  6.15 us

profile of v8, /device:TPU:0, one launch (start us, length us, event | category | flops | bytes accessed | tf_op | source)
XLA Modules:
  0.0 43.9 jit_solution(2710031538103727438)
XLA Ops:
  0.6 37.0 %stats.1 = (f32[2,1680,640]{2,1,0:T(8,128)S(1)}, f32[2,640]{1,0:T(2,128)S(1)}, f32[2,1680]{1,0:T(2,128)S(1)}, f32[2,1680,640]{2,1,0:T(8,128)S(1)}, f32[2,1680]{1...) custom-call(f32[3]{0:T(128)} %hyper.1, f32[2,1680,640]{2,1,0:T(8,128)} %bitcast.6, ...), custom_call_target="tpu_custom_call" | custom-call | tf_op jit(solution)/shard_map/stats/pallas_call | solution.py:319
  37.6 6.1 %write.1 = (f32[2,1680,640]{2,1,0:T(8,128)}, f32[2,640]{1,0:T(2,128)}, f32[2,1680]{1,0:T(2,128)}, f32[2,1680,640]{2,1,0:T(8,128)}, f32[2,1680]{1,0:T(2,128)}, /*...) custom-call(f32[2,1680,640]{2,1,0:T(8,128)S(1)} %get-tuple-element.20.refs_0_, ...), custom_call_target="tpu_custom_call", output_to_operand_aliasing={{6}: (6, {})} | custom-call | tf_op jit(solution)/shard_map/write/pallas_call | solution.py:345
